TPU v7x, 512 devices: a whole 4x8x8 slice. The times are simulated.
512 devices in a mesh: dp: 32 (over y, x), mp: 16 (over z, core).
Axes of the slice: x: 4, y: 8, z: 8, core: 2. Of those that a mesh axis runs over, the one named last changes fastest.
Arguments:
- buffer: bfloat16 [1048576, 256], P(('dp', 'mp')), may hold values from -24 to 24, as said below
- owner: int32 [524288, 1], P(('dp', 'mp')), may hold values from 0 to 511; in each aligned block of 1024 rows (0 to 1023, 1024 to 2047, ...) at most 8 rows name the same one
- local_row: int32 [524288], P(('dp', 'mp')), may hold values from 0 to 2047
- q_in: bfloat16 [2, 130, 256], replicated, may hold values from -0.5 to 0.5
- q_mid: bfloat16 [2, 256, 256], replicated, may hold values from -0.5 to 0.5
- q_out: bfloat16 [2, 256], replicated, may hold values from -0.5 to 0.5
- v_in: bfloat16 [124, 256], replicated, may hold values from -0.5 to 0.5
- v_mid: bfloat16 [256, 256], replicated, may hold values from -0.5 to 0.5
- v_out: bfloat16 [256], replicated, may hold values from -0.5 to 0.5
Outputs:
- q_values: float32 [2, 524288], P(None, ('dp', 'mp'))
- values: float32 [2, 524288], P(None, ('dp', 'mp'))
- targets: float32 [524288], P(('dp', 'mp'))
- q_loss: float32 [524288], P(('dp', 'mp'))
- value_loss: float32 [524288], P(('dp', 'mp'))
Inputs may be any that keep to these rules, and one draw needn't show every extreme that they name: Owner o is the replay owner at position o of the devices in dp+mp order. In the rows of one reader no owner is named more than 8 times, a bound that some block reaches. `buffer`: action values lie in -1 to 1 and discounts in 0 to 0.99.
All inputs are finite; a program needn't handle non-finite values.
Results may differ from a plain program's by a relative error of at most 0.005.
Values may be sent and summed in bfloat16 or wider, within the bound.
No kernel may reach another device: no remote copies, remote signals or barrier semaphores. Data moves between devices by JAX's collectives and lax.ppermute only.
A program may use at most 64 MiB of HBM per device.

v0:
```python
import jax
import jax.numpy as jnp
from jax import lax
from jax.sharding import PartitionSpec as P


def split_up(array, dim, length):
    dims = array.shape
    tiles = array.reshape(*dims[:dim], length, dims[dim] // length, *dims[dim + 1 :])
    return jnp.moveaxis(tiles, dim, 0)


def laid_out(tiles, dim):
    tiles = jnp.moveaxis(tiles, 0, dim)
    dims = tiles.shape
    return tiles.reshape(*dims[:dim], dims[dim] * dims[dim + 1], *dims[dim + 2 :])


def exchange_both(array, axis, axes, splits, concats):
    sizes = [lax.axis_size(a) for a in axes]
    tiles = split_up(array, splits[0], sizes[0])
    tiles = jnp.moveaxis(split_up(tiles, splits[1] + 1, sizes[1]), 0, 1)
    inside = tiles.shape[2:]
    tiles = tiles.reshape(-1, *inside)
    tiles = lax.all_to_all(tiles, axis, split_axis=0, concat_axis=0, tiled=True)
    tiles = laid_out(tiles.reshape(*sizes, *inside), concats[0] + 1)
    return laid_out(tiles, concats[1])


def layer_two(first, mid, out):
    hidden = jnp.maximum(jnp.dot(first, mid, preferred_element_type=jnp.float32), 0.0)
    return jnp.dot(hidden, out.astype(jnp.float32), precision=lax.Precision.HIGHEST)


def critic_block(rows, weights, states_width, pair_width):
    q_in, q_mid, q_out, v_in, v_mid, v_out = weights
    pair = rows[:, :pair_width]
    state = rows[:, :states_width]
    nexts = rows[:, pair_width : pair_width + states_width]
    reward = rows[:, pair_width + states_width].astype(jnp.float32)
    discount = rows[:, pair_width + states_width + 1].astype(jnp.float32)
    first_one = jnp.maximum(jnp.dot(pair, q_in[0], preferred_element_type=jnp.float32), 0.0).astype(
        jnp.bfloat16
    )
    first_two = jnp.maximum(jnp.dot(pair, q_in[1], preferred_element_type=jnp.float32), 0.0).astype(
        jnp.bfloat16
    )
    q_first = layer_two(first_one, q_mid[0], q_out[0])
    q_second = layer_two(first_two, q_mid[1], q_out[1])
    both = jnp.concatenate([state, nexts], axis=0)
    first_value = jnp.maximum(jnp.dot(both, v_in, preferred_element_type=jnp.float32), 0.0).astype(
        jnp.bfloat16
    )
    value_all = layer_two(first_value, v_mid, v_out)
    count = state.shape[0]
    value_now = value_all[:count]
    value_next = value_all[count:]
    targets = reward + discount * value_next
    return (q_first, q_second, value_now, value_next, targets)


def body(buffer, owner, local_row, q_in, q_mid, q_out, v_in, v_mid, v_out):
    outer = lax.axis_size("dp")
    inner = lax.axis_size("mp")
    owners = outer * inner
    batch = local_row.shape[0]
    columns_all = buffer.shape[1]
    states_width = v_in.shape[0]
    pair_width = q_in.shape[1]
    weights = (q_in, q_mid, q_out, v_in, v_mid, v_out)
    slots_each = max(2, 4 * batch // owners)
    target_owner = owner[:, 0]
    positions = jnp.arange(batch, dtype=jnp.int32)
    same_owner = target_owner[:, None] == target_owner[None, :]
    earlier = positions[None, :] < positions[:, None]
    placed = jnp.sum(jnp.logical_and(same_owner, earlier).astype(jnp.int32), axis=1)
    slot = target_owner * slots_each + placed
    owner_hot = (target_owner[:, None] == jnp.arange(owners, dtype=jnp.int32)[None, :]).astype(
        jnp.float32
    )
    place_hot = (placed[:, None] == jnp.arange(slots_each, dtype=jnp.int32)[None, :]).astype(
        jnp.float32
    )
    weighted = place_hot * (local_row.astype(jnp.float32) + 1.0)[:, None]
    table = jnp.dot(owner_hot.T, weighted, precision=lax.Precision.HIGHEST)
    requests = (table.astype(jnp.int32) - 1).reshape(outer, inner, slots_each)
    asked = exchange_both(requests, ("dp", "mp"), ("dp", "mp"), (0, 1), (0, 1))
    picked = jnp.take(buffer, jnp.maximum(asked, 0).reshape(-1), axis=0)
    answered = exchange_both(
        picked.reshape(outer, inner, slots_each, columns_all),
        ("dp", "mp"),
        ("dp", "mp"),
        (0, 1),
        (0, 1),
    )
    rows = jnp.take(answered.reshape(owners * slots_each, columns_all), slot, axis=0)
    q_first, q_second, value_now, value_next, targets = critic_block(
        rows, weights, states_width, pair_width
    )
    q_loss = (q_first - targets) ** 2 + (q_second - targets) ** 2
    gap = jnp.minimum(q_first, q_second) - value_now
    value_loss = jnp.where(gap < 0.0, 0.3, 0.7) * gap * gap
    return (
        jnp.stack([q_first, q_second]),
        jnp.stack([value_now, value_next]),
        targets,
        q_loss,
        value_loss,
    )


def solution(mesh):
    return jax.shard_map(
        body,
        mesh=mesh,
        in_specs=(
            P(("dp", "mp"), None),
            P(("dp", "mp"), None),
            P(("dp", "mp")),
            P(),
            P(),
            P(),
            P(),
            P(),
            P(),
        ),
        out_specs=(
            P(None, ("dp", "mp")),
            P(None, ("dp", "mp")),
            P(("dp", "mp")),
            P(("dp", "mp")),
            P(("dp", "mp")),
        ),
        check_vma=False,
    )
```

profile of v0, /device:TPU:1, one launch (start us, length us, event | category | flops | bytes accessed | tf_op | source)
XLA Modules:
  0.0 143.2 jit_solution(5318049415892928874)
XLA Ops:
  0.6 0.0 copy-start
  0.6 1.3 convert_reduce_fusion
  2.0 0.7 convert_add_fusion
  2.6 1.8 %fusion.7 = s32[512,1,1,8]{0,3,2,1:T(8,128)S(1)} fusion(s32[1024]{0:T(1024)} %bitcast.80, f32[1024]{0:T(1024)S(1)} %convert_add_fusion, s32[1024]{0:T(1024)S(1)} %convert_reduce_fusion), kind=kOutput, calls=%fused_computation.19 | convolution fusion | flops 50880512 | bytes 28672 | tf_op jit(solution)/shard_map/dot_general | solution.py:85
  4.4 0.1 copy.33
  4.5 39.3 %all_to_all.10 = s32[512,1,1,8]{3,2,1,0:T(1,128)S(1)} all-to-all(s32[512,1,1,8]{3,2,1,0:T(1,128)S(1)} %copy.33), channel_id=1, replica_groups=mesh['dp'=32,'mp'=16] {'dp','mp'}, dimensions={0} | all-to-all | bytes 32768 | tf_op jit(solution)/shard_map/all_to_all | solution.py:25
  43.9 0.1 copy.34
  44.0 0.1 reshape.85
  44.1 0.1 copy.36
  44.3 0.1 reshape.90
  44.4 0.2 copy.40
  44.6 0.0 copy-done
  44.6 14.6 %gather_fusion = bf16[4096,256]{1,0:T(8,128)(2,1)S(1)} fusion(bf16[2048,256]{1,0:T(8,128)(2,1)S(1)} %copy-done, s32[4096]{0:T(1024)S(1)} %broadcast_clamp_fusion), kind=kCustom, calls=%fused_computation | custom fusion | bytes 4210688 | tf_op jit(solution)/shard_map/jit(_take)/gather | solution.py:88
  59.2 1.7 %bitcast_select_fusion = bf16[512,1,1,8,256]{4,3,2,1,0:T(8,128)(2,1)} fusion(bf16[4096,256]{1,0:T(8,128)(2,1)S(1)} %gather_fusion, pred[512,8]{1,0:T(8,128)(4,1)S(1)} %bitcast.72), kind=kLoop, calls=%fused_computation.8 | loop fusion | flops 1048576 | bytes 4198400 | tf_op jit(solution)/shard_map/jit(_take)/select_n | solution.py:88
  61.0 0.0 copy-start.8
  61.0 0.0 copy-start.6
  61.0 0.0 copy-start.1
  61.0 8.7 %all-to-all-start.1 = ((bf16[512,1,1,8,256]{4,3,2,1,0:T(8,128)(2,1)}), bf16[512,1,1,8,256]{4,3,2,1,0:T(8,128)(2,1)S(1)}, u32[]{:S(2)}, u32[]{:S(2)}) async-start(bf16[512,1,1,8,256]{4,3,2,1,0:T(8,128)(2,1)} %bitcast_select_fusion), calls=%async_computation.1 | async-start | bytes 4194304 | tf_op jit(solution)/shard_map/all_to_all | solution.py:25
  69.7 0.0 copy-done.8
  69.7 0.6 reshape.109
  70.3 0.0 copy-done.6
  70.3 0.6 and_reduce_fusion
  70.9 0.0 copy-done.1
  70.9 0.2 fusion.44
  71.1 54.0 %all-to-all-done.1 = bf16[512,1,1,8,256]{4,3,2,1,0:T(8,128)(2,1)S(1)} async-done(((bf16[512,1,1,8,256]{4,3,2,1,0:T(8,128)(2,1)}), bf16[512,1,1,8,256]{4,3,2,1,0:T(8,128)(2,1)S(1)}, u32[]{:S(2)}, u32[]{:S(2)}) %all-to-all-start.1) | async-done | bytes 2097184 | tf_op jit(solution)/shard_map/all_to_all | solution.py:25
  125.1 0.0 copy-start.5
  125.1 4.9 %gather_fusion.1 = bf16[1024,256]{1,0:T(8,128)(2,1)} fusion(bf16[4096,256]{1,0:T(8,128)(2,1)S(1)} %bitcast.70, s32[1024]{0:T(1024)S(1)} %broadcast_clamp_fusion.1), kind=kCustom, calls=%fused_computation.1 | custom fusion | bytes 1052672 | tf_op jit(solution)/shard_map/jit(_take)/gather | solution.py:96
  130.0 0.0 copy-done.5
  130.0 1.2 broadcast_select_fusion
  131.2 0.0 copy-start.7
  131.3 0.8 fusion.43
  132.1 0.0 copy-start.4
  132.1 1.0 convert_reduce_fusion.1
  133.1 1.4 convolution_maximum_fusion.3
  134.5 0.0 copy-start.2
  134.5 0.0 copy-done.7
  134.5 1.5 %convolution_maximum_fusion.2 = f32[1024,256]{1,0:T(8,128)} fusion(bf16[1024,256]{1,0:T(8,128)(2,1)S(1)} %broadcast_select_fusion, bf16[2,256,256]{2,1,0:T(8,128)(2,1)S(1)} %copy-done.7, bf16[1,130,256]{2,0,1:T(2,128)(2,1)S(1)} %get-tuple-element.14), kind=kOutput, calls=%fused_computation.11 | convolution fusion | flops 203161600 | bytes 1837056 | tf_op jit(solution)/shard_map/dot_general | solution.py:31
  136.0 0.0 copy-done.4
  136.0 0.6 fusion.33
  136.6 1.8 %fusion.31 = f32[1,1024]{1,0:T(1,128)S(1)} fusion(f32[1024,256]{1,0:T(8,128)} %convolution_maximum_fusion.2, bf16[2,256]{1,0:T(2,128)(2,1)S(1)} %copy-done.4), kind=kOutput, calls=%fused_computation.57 | convolution fusion | flops 3145728 | bytes 1053696 | tf_op jit(solution)/shard_map/dot_general | solution.py:32
  138.4 0.0 copy-done.2
  138.4 0.0 copy-start.3
  138.4 1.8 %convolution_maximum_fusion = f32[2048,256]{1,0:T(8,128)S(1)} fusion(bf16[256,256]{1,0:T(8,128)(2,1)S(1)} %copy-done.2, bf16[124,256]{1,0:T(8,128)(2,1)} %param.15, bf16[1024,124]{1,0:T(8,128)(2,1)} %get-tuple-element.12, bf16[1024,124]{1,0:T(8,128)(2,1)S(1)} %get-tuple-element.11), kind=kOutput, calls=%fused_computation.5 | convolution fusion | flops 401047552 | bytes 2799616 | tf_op jit(solution)/shard_map/dot_general | solution.py:31
  140.2 1.7 %fusion.45 = f32[1,2048]{1,0:T(1,128)S(1)} fusion(f32[2048,256]{1,0:T(8,128)S(1)} %convolution_maximum_fusion, bf16[256,1]{0,1:T(2,128)(2,1)} %reshape.109), kind=kOutput, calls=%fused_computation.70 | convolution fusion | flops 6291456 | bytes 2105856 | tf_op jit(solution)/shard_map/dot_general | solution.py:32
  141.9 0.0 copy-done.3
  141.9 0.6 multiply_add_fusion
  142.6 0.6 pad_maximum_fusion
  (4 shorter events, 0.0 us)
Async XLA Ops:
  0.6 44.0 %copy-start = (bf16[2048,256]{1,0:T(8,128)(2,1)S(1)}, bf16[2048,256]{1,0:T(8,128)(2,1)}, u32[]{:S(2)}) copy-start(bf16[2048,256]{1,0:T(8,128)(2,1)} %param.9) | copy-start | bytes 3145732
  61.0 8.7 %copy-start.8 = (bf16[256]{0:T(256)(128)(2,1)S(1)}, bf16[256]{0:T(256)(128)(2,1)}, u32[]{:S(2)}) copy-start(bf16[256]{0:T(256)(128)(2,1)} %param.17) | copy-start | bytes 1540
  61.0 9.3 %copy-start.6 = (s32[1024,1]{0,1:T(1,128)S(1)}, s32[1024,1]{0,1:T(1,128)}, u32[]{:S(2)}) copy-start(s32[1024,1]{0,1:T(1,128)} %param.10) | copy-start | bytes 12292
  61.0 9.9 %copy-start.1 = (bf16[2,130,256]{2,0,1:T(2,128)(2,1)S(1)}, bf16[2,130,256]{2,0,1:T(2,128)(2,1)}, u32[]{:S(2)}) copy-start(bf16[2,130,256]{2,0,1:T(2,128)(2,1)} %param.12) | copy-start | bytes 399364
  61.0 64.1 %all-to-all-start.1 = ((bf16[512,1,1,8,256]{4,3,2,1,0:T(8,128)(2,1)}), bf16[512,1,1,8,256]{4,3,2,1,0:T(8,128)(2,1)S(1)}, u32[]{:S(2)}, u32[]{:S(2)}) async-start(bf16[512,1,1,8,256]{4,3,2,1,0:T(8,128)(2,1)} %bitcast_select_fusion), calls=%async_computation.1 | async-start | bytes 4194304 | tf_op jit(solution)/shard_map/all_to_all | solution.py:25
  125.1 4.9 %copy-start.5 = (pred[1024]{0:T(1024)(128)(4,1)S(1)}, pred[1024]{0:T(1024)(128)(4,1)}, u32[]{:S(2)}) copy-start(pred[1024]{0:T(1024)(128)(4,1)} %get-tuple-element.9) | copy-start | bytes 3076
  131.2 3.3 %copy-start.7 = (bf16[2,256,256]{2,1,0:T(8,128)(2,1)S(1)}, bf16[2,256,256]{2,1,0:T(8,128)(2,1)}, u32[]{:S(2)}) copy-start(bf16[2,256,256]{2,1,0:T(8,128)(2,1)} %param.13) | copy-start | bytes 786436
  132.1 3.9 %copy-start.4 = (bf16[2,256]{1,0:T(2,128)(2,1)S(1)}, bf16[2,256]{1,0:T(2,128)(2,1)}, u32[]{:S(2)}) copy-start(bf16[2,256]{1,0:T(2,128)(2,1)} %param.14) | copy-start | bytes 3076
  134.5 3.9 %copy-start.2 = (bf16[256,256]{1,0:T(8,128)(2,1)S(1)}, bf16[256,256]{1,0:T(8,128)(2,1)}, u32[]{:S(2)}) copy-start(bf16[256,256]{1,0:T(8,128)(2,1)} %param.16) | copy-start | bytes 393220
  138.4 3.5 %copy-start.3 = (f32[1024]{0:T(1024)S(1)}, f32[1024]{0:T(1024)}, u32[]{:S(2)}) copy-start(f32[1024]{0:T(1024)} %get-tuple-element.6) | copy-start | bytes 12292
where the time goes:
time: 144 us; the launch traced here: 143 us
  waiting for transfers between devices  54 us (38%)
  blocking collectives  39.3 us (27%)
  local copies, waits for them, and re-layouts  22 us (15%)
  matrix products  10.6 us (7%)
  starting transfers between devices  8.7 us (6%)
  other arithmetic  7.81 us (5%)
    all_to_all x1, waiting for transfers between devices, exchange_both(): tiles = lax.all_to_all(tiles, axis, split_axis=0, concat_axis=0, tiled=True)  54 us
    all_to_all x1, blocking collectives, exchange_both(): tiles = lax.all_to_all(tiles, axis, split_axis=0, concat_axis=0, tiled=True)  39.3 us
    gather x1, local copies, waits for them, and re-layouts, body(): picked = jnp.take(buffer, jnp.maximum(asked, 0).reshape(-1), axis=0)  14.6 us
    all_to_all x1, starting transfers between devices, exchange_both(): tiles = lax.all_to_all(tiles, axis, split_axis=0, concat_axis=0, tiled=True)  8.7 us
    gather x1, local copies, waits for them, and re-layouts, body(): jnp.take(answered.reshape(owners * slots_each, columns_all), slot, axis=0)  4.94 us
    dot_general x3, matrix products, layer_two(): jnp.dot(first, mid, preferred_element_type=jnp.float32)  4.71 us
    dot_general x3, matrix products, layer_two(): jnp.dot(hidden, out.astype(jnp.float32), precision=lax.Precision.HIGHEST)  4.13 us
  transfers between devices with their start and end apart: 1, of which 1 were waited for; matrix products, arithmetic and copies ran while one was open for 1% of the time, Pallas kernels for 0%

commit v1 on v0

v1 whole, which is shorter than its diff:
```python
import jax
import jax.numpy as jnp
from jax import lax
from jax.experimental import pallas as pl
from jax.experimental.pallas import tpu as pltpu
from jax.sharding import Mesh
from jax.sharding import PartitionSpec as P

FAR = ("y", "z")
SIDE = ("x", "c")
SLOTS = 8
NV = 5
F32 = jnp.float32
BF16 = jnp.bfloat16
I32 = jnp.int32
SMALL = pltpu.CompilerParams(vmem_limit_bytes=16 * 2**20)


def split_owner(owner):
    y = owner >> 6
    x = (owner >> 4) & 3
    z = (owner >> 1) & 7
    c = owner & 1
    return y * 8 + z, x * 2 + c


def iota(shape, dim):
    return lax.broadcasted_iota(I32, shape, dim)


def nt(a, b):
    return lax.dot_general(a, b, (((1,), (1,)), ((), ())), preferred_element_type=F32)


def tn(a, b):
    return lax.dot_general(a, b, (((0,), (0,)), ((), ())), preferred_element_type=F32)


def request_kernel(owner_ref, local_ref, request_ref, rank_ref):
    chunks = owner_ref.shape[0]
    owner = owner_ref[...]
    columns = jnp.transpose(owner.astype(F32), (1, 0))
    before = iota((128, 128), 0) < iota((128, 128), 1)
    rows = [owner_ref[k : k + 1, :].astype(F32) for k in range(chunks)]
    totals = [jnp.zeros((128, 128), F32) for _ in range(chunks)]
    for q in range(chunks):
        column = jnp.broadcast_to(columns[:, q : q + 1], (128, 128))
        for k in range(q, chunks):
            same = column == rows[k]
            if k == q:
                same = jnp.logical_and(same, before)
            totals[k] = totals[k] + jnp.where(same, 1.0, 0.0)
    high = jnp.zeros((64, 128), F32)
    low = jnp.zeros((64, 128), F32)
    for k in range(chunks):
        rank = jnp.sum(totals[k], axis=0, keepdims=True).astype(I32)
        rank_ref[k : k + 1, :] = rank
        far, side = split_owner(owner_ref[k : k + 1, :])
        local = local_ref[k : k + 1, :]
        place = iota((128, 128), 0) == side * SLOTS + rank
        target = jnp.where(iota((64, 128), 0) == far, 1.0, 0.0).astype(BF16)
        high = high + nt(target, jnp.where(place, (local >> 7).astype(F32), 0.0).astype(BF16))
        low = low + nt(target, jnp.where(place, (local & 127).astype(F32), 0.0).astype(BF16))
    wanted = high.astype(I32) * 128 + low.astype(I32)
    request_ref[...] = wanted.reshape(64, 1, 128)


def critic_kernel(
    rows_ref, q0_ref, q1_ref, q_mid_ref, q_out_ref, v_in_ref, v_mid_ref, v_out_ref,
    table_ref, first_ref, mid_ref,
):
    count, width = rows_ref.shape
    states = v_in_ref.shape[0]
    pair = q0_ref.shape[0]

    def spread(weights, offset):
        inner = weights.shape[0]
        place = jnp.where(iota((inner, width), 1) == iota((inner, width), 0) + offset, 1.0, 0.0)
        return tn(weights, place.astype(BF16)).astype(BF16)

    first_ref[0:256, :] = spread(q0_ref[...], 0)
    first_ref[256:512, :] = spread(q1_ref[...], 0)
    first_ref[512:768, :] = spread(v_in_ref[...], 0)
    first_ref[768:1024, :] = spread(v_in_ref[...], pair)
    mid_ref[0] = spread(q_mid_ref[0], 0)
    mid_ref[1] = spread(q_mid_ref[1], 0)
    mid_ref[2] = spread(v_mid_ref[...], 0)
    unit = jnp.where(iota((256, 256), 0) == iota((256, 256), 1), 1.0, 0.0)

    def as_column(row):
        return jnp.sum(unit * row.astype(F32), axis=1, keepdims=True)

    outs = [as_column(q_out_ref[0:1, :]), as_column(q_out_ref[1:2, :]), as_column(v_out_ref[...])]
    outs = [jnp.broadcast_to(o, (256, 128)) for o in outs]
    tail = jnp.where(
        iota((8, width), 1) == iota((8, width), 0) + (pair + states), 1.0, 0.0
    ).astype(BF16)
    block = 256
    for b in range(count // block):
        x = rows_ref[b * block : (b + 1) * block, :]
        first = jnp.maximum(nt(first_ref[...], x), 0.0).astype(BF16)
        ends = nt(tail, x)
        results = []
        for i in range(4):
            m = min(i, 2)
            hidden = jnp.dot(
                mid_ref[m], first[i * 256 : (i + 1) * 256, :], preferred_element_type=F32
            )
            hidden = jnp.maximum(hidden, 0.0)
            weight = jnp.concatenate([outs[m]] * (block // 128), axis=1)
            results.append(jnp.sum(hidden * weight, axis=0, keepdims=True))
        target = ends[0:1, :] + ends[1:2, :] * results[3]
        results.append(target)
        for v in range(NV):
            for half in range(block // 128):
                row = v * 16 + b * (block // 128) + half
                piece = results[v][:, half * 128 : (half + 1) * 128]
                for s in range(8):
                    table_ref[s, row : row + 1, :] = piece


def serve_kernel(tables_ref, request_ref, answer_ref):
    wanted = request_ref[...].reshape(64, 128)
    expand = jnp.where(iota((64, 512), 0) == iota((64, 512), 1) // SLOTS, 1.0, 0.0).astype(BF16)
    own = iota((128, 512), 0) % SLOTS == iota((128, 512), 1) % SLOTS
    gather_side = jnp.where(iota((8, 128), 0) == iota((8, 128), 1) // SLOTS, 1.0, 0.0).astype(BF16)

    def by_side(values):
        wide = jnp.where(own, tn(values.astype(F32).astype(BF16), expand), 0.0).astype(BF16)
        return jnp.dot(gather_side, wide, preferred_element_type=F32).astype(I32)

    high = by_side(wanted >> 7)
    low = by_side(wanted & 127)
    lane_block = iota((8, 128), 1) // SLOTS
    for c in range(4):
        high_c = high[:, c * 128 : (c + 1) * 128]
        low_c = low[:, c * 128 : (c + 1) * 128]
        found = [jnp.zeros((8, 128), F32) for _ in range(NV)]
        for k in range(16):
            here = high_c == k
            for v in range(NV):
                piece = tables_ref[:, v * 16 + k, :]
                found[v] = jnp.where(here, jnp.take_along_axis(piece, low_c, axis=1), found[v])
        found = [found[0]] + [pltpu.roll(found[v], v * SLOTS, 1) for v in range(1, NV)]
        for h in range(16):
            message = found[0]
            for v in range(1, NV):
                message = jnp.where(lane_block == (h + v) % 16, found[v], message)
            if h:
                message = pltpu.roll(message, 128 - h * SLOTS, 1)
            answer_ref[c * 16 + h] = message


def finish_kernel(
    answer_ref, owner_ref, rank_ref, q_ref, values_ref, target_ref, q_loss_ref, value_loss_ref
):
    answers = answer_ref[...].reshape(512, 128)
    part_one = answers.astype(BF16)
    rest = answers - part_one.astype(F32)
    part_two = rest.astype(BF16)
    part_three = (rest - part_two.astype(F32)).astype(BF16)
    parts = [jnp.transpose(p, (1, 0))[: NV * SLOTS, :] for p in (part_one, part_two, part_three)]
    for k in range(owner_ref.shape[0]):
        far, side = split_owner(owner_ref[k : k + 1, :])
        hot = jnp.where(iota((512, 128), 0) == far * 8 + side, 1.0, 0.0).astype(BF16)
        got = jnp.dot(parts[0], hot, preferred_element_type=F32)
        got = got + jnp.dot(parts[1], hot, preferred_element_type=F32)
        got = got + jnp.dot(parts[2], hot, preferred_element_type=F32)
        mine = iota((8, 128), 0) == rank_ref[k : k + 1, :]
        q0, q1, now, later, target = [
            jnp.sum(
                jnp.where(mine, got[v * SLOTS : (v + 1) * SLOTS, :], 0.0), axis=0, keepdims=True
            )
            for v in range(NV)
        ]
        span = slice(k * 128, (k + 1) * 128)
        q_ref[0:1, span] = q0
        q_ref[1:2, span] = q1
        values_ref[0:1, span] = now
        values_ref[1:2, span] = later
        target_ref[:, span] = target
        q_loss_ref[:, span] = (q0 - target) ** 2 + (q1 - target) ** 2
        gap = jnp.minimum(q0, q1) - now
        value_loss_ref[:, span] = jnp.where(gap < 0.0, 0.3, 0.7) * gap * gap


def shape(dims, dtype):
    return jax.ShapeDtypeStruct(dims, dtype)


def make_request(owner, local_row):
    return pl.pallas_call(
        request_kernel,
        out_shape=(shape((64, 1, 128), I32), shape((8, 128), I32)),
        compiler_params=SMALL,
        name="make_request",
    )(owner, local_row)


def critics(buffer, q_in, q_mid, q_out, v_in, v_mid, v_out):
    return pl.pallas_call(
        critic_kernel,
        out_shape=shape((8, NV * 16, 128), F32),
        scratch_shapes=[pltpu.VMEM((1024, 256), BF16), pltpu.VMEM((3, 256, 256), BF16)],
        cost_estimate=pl.CostEstimate(
            flops=2 * 2048 * 1024 * 512, bytes_accessed=2_000_000, transcendentals=0
        ),
        compiler_params=SMALL,
        name="critics",
    )(buffer, q_in[0], q_in[1], q_mid, q_out, v_in, v_mid, v_out.reshape(1, -1))


def serve(tables, requests):
    return pl.pallas_call(
        serve_kernel, out_shape=shape((64, 8, 128), F32), compiler_params=SMALL, name="serve"
    )(tables, requests)


def finish(answers, owner, rank):
    line = shape((1, 1024), F32)
    two = shape((2, 1024), F32)
    return pl.pallas_call(
        finish_kernel, out_shape=(two, two, line, line, line), compiler_params=SMALL, name="finish"
    )(answers, owner, rank)


def body(buffer, owner, local_row, q_in, q_mid, q_out, v_in, v_mid, v_out):
    owner = owner.reshape(8, 128)
    local_row = local_row.reshape(8, 128)
    requests, rank = make_request(owner, local_row)
    requests = lax.all_to_all(requests, FAR, 0, 0, tiled=True)
    table = critics(buffer, q_in, q_mid, q_out, v_in, v_mid, v_out)
    tables = lax.all_to_all(table, SIDE, 0, 0, tiled=True)
    answers = serve(tables, requests)
    answers = lax.all_to_all(answers, FAR, 0, 0, tiled=True)
    q_values, values, targets, q_loss, value_loss = finish(answers, owner, rank)
    return q_values, values, targets.reshape(-1), q_loss.reshape(-1), value_loss.reshape(-1)


def solution(mesh):
    fine = Mesh(mesh.devices.reshape(8, 4, 8, 2), ("y", "x", "z", "c"))
    every = ("y", "x", "z", "c")
    return jax.shard_map(
        body,
        mesh=fine,
        in_specs=(P(every, None), P(every, None), P(every), P(), P(), P(), P(), P(), P()),
        out_specs=(P(None, every), P(None, every), P(every), P(every), P(every)),
        check_vma=False,
    )
```

time: 144 us -> 69.1 us (0.48)
  waiting for transfers between devices: 54 us -> 3.81 us
  local copies, waits for them, and re-layouts: 22 us -> 4.79 us
  matrix products: 10.6 us -> 0 us
  starting transfers between devices: 8.7 us -> 17.1 us
  Pallas kernels: 0 us -> 7.85 us
  other arithmetic: 7.81 us -> 0 us
  blocking collectives: 39.3 us -> 33.5 us
    all_to_all x1, waiting for transfers between devices: 54 us -> 3.81 us  [body(): requests = lax.all_to_all(requests, FAR, 0, 0, tiled=True)]
    gather x2 -> x0, local copies, waits for them, and re-layouts: 19.6 us -> none  [the longest x1 14.6 us: body(): picked = jnp.take(buffer, jnp.maximum(asked, 0).reshape(-1), axis=0)]
    dot_general x7 -> x0, matrix products: 10.6 us -> none  [the longest x3 4.71 us: layer_two(): jnp.dot(first, mid, preferred_element_type=jnp.float32)]
    all_to_all x1, starting transfers between devices: 8.7 us -> 17.1 us  [body(): requests = lax.all_to_all(requests, FAR, 0, 0, tiled=True)]
    pallas_call x0 -> x4, Pallas kernels: none -> 7.85 us  [the longest x1 3.57 us: critics(): pl.pallas_call(critic_kernel, out_shape=shape((8, NV * 16, 128), F32), sc...]
    all_to_all x1 -> x2, blocking collectives: 39.3 us -> 33.5 us  [the longest x1 19.8 us: body(): answers = lax.all_to_all(answers, FAR, 0, 0, tiled=True)]
    select_n x2 -> x0, other arithmetic: 2.98 us -> none  [the longest x1 1.73 us: body(): picked = jnp.take(buffer, jnp.maximum(asked, 0).reshape(-1), axis=0)]
    unnamed x19 -> x18, local copies, waits for them, and re-layouts: 0.61 us -> 3.53 us
  transfers between devices with their start and end apart: 1 -> 1, of which waited for: 1 -> 1; matrix products, arithmetic and copies ran while one was open for 1% -> 2% of each run, Pallas kernels for 0% -> 5%
where the time goes in v1:
time: 69.1 us; the launch traced here: 67.8 us
  blocking collectives  33.5 us (48%)
  starting transfers between devices  17.1 us (25%)
  Pallas kernels  7.85 us (11%)
  local copies, waits for them, and re-layouts  4.79 us (7%)
  waiting for transfers between devices  3.81 us (6%)
  between operations  0.75 us (1%)
    all_to_all x1, blocking collectives, body(): answers = lax.all_to_all(answers, FAR, 0, 0, tiled=True)  19.8 us
    all_to_all x1, starting transfers between devices, body(): requests = lax.all_to_all(requests, FAR, 0, 0, tiled=True)  17.1 us
    all_to_all x1, blocking collectives, body(): tables = lax.all_to_all(table, SIDE, 0, 0, tiled=True)  13.6 us
    all_to_all x1, waiting for transfers between devices, body(): requests = lax.all_to_all(requests, FAR, 0, 0, tiled=True)  3.81 us
    pallas_call x1, Pallas kernels, critics(): pl.pallas_call(critic_kernel, out_shape=shape((8, NV * 16, 128), F32), sc...  3.57 us
    unnamed x18, local copies, waits for them, and re-layouts  3.53 us
    pallas_call x1, Pallas kernels, serve(): pl.pallas_call(serve_kernel, out_shape=shape((64, 8, 128), F32), compiler...  1.62 us
  transfers between devices with their start and end apart: 1, of which 1 were waited for; matrix products, arithmetic and copies ran while one was open for 2% of the time, Pallas kernels for 5%

profile of v1, /device:TPU:1, one launch (start us, length us, event | category | flops | bytes accessed | tf_op | source)
XLA Modules:
  0.0 67.8 jit_solution(6013566558883443226)
XLA Ops:
  0.6 0.0 copy-start
  0.6 0.7 copy-done
  1.3 0.0 copy-start.2
  1.3 0.7 %copy-done.2 = s32[1024]{0:T(1024)S(1)} copy-done((s32[1024]{0:T(1024)S(1)}, s32[1024]{0:T(1024)}, u32[]{:S(2)}) %copy-start.2) | copy-done | bytes 4120
  2.0 1.4 %make_request.1 = (s32[64,1,128]{2,1,0:T(1,128)}, s32[8,128]{1,0:T(8,128)S(1)}) custom-call(s32[8,128]{1,0:T(8,128)S(1)} %bitcast.9, s32[8,128]{1,0:T(8,128)S(1)} %bitcast.11), custom_call_target="tpu_custom_call" | custom-call | tf_op jit(solution)/shard_map/make_request/pallas_call | solution.py:192
  3.4 17.1 %all-to-all-start.1 = ((s32[64,1,128]{2,1,0:T(1,128)}), s32[64,1,128]{2,1,0:T(1,128)S(1)}, u32[]{:S(2)}, u32[]{:S(2)}) async-start(s32[64,1,128]{2,1,0:T(1,128)} %get-tuple-element.12), calls=%async_computation.1 | async-start | bytes 65536 | tf_op jit(solution)/shard_map/all_to_all | solution.py:231
  20.5 0.0 copy-start.8
  20.5 0.0 copy-start.6
  20.5 1.2 %fusion = (bf16[1,130,256]{2,0,1:T(2,128)(2,1)S(1)}, bf16[1,130,256]{2,0,1:T(2,128)(2,1)S(1)}) fusion(bf16[2,130,256]{2,0,1:T(2,128)(2,1)} %param.12), kind=kLoop, calls=%fused_computation.2 | loop fusion | bytes 266240 | tf_op jit(solution)/shard_map/slice | solution.py:210
  21.8 0.0 copy-done.8
  21.8 0.0 copy-start.4
  21.8 0.0 copy-start.5
  21.9 0.0 copy-start.7
  21.9 0.0 copy-done.6
  21.9 0.9 %copy-done.4 = bf16[2,256,256]{2,1,0:T(8,128)(2,1)S(1)} copy-done((bf16[2,256,256]{2,1,0:T(8,128)(2,1)S(1)}, bf16[2,256,256]{2,1,0:T(8,128)(2,1)}, u32[]{:S(2)}) %copy-start.4) | copy-done | bytes 262168
  22.7 0.0 copy-done.5
  22.8 0.0 copy-done.7
  22.8 0.0 copy-start.3
  22.8 1.2 %copy-done.3 = bf16[2048,256]{1,0:T(8,128)(2,1)S(1)} copy-done((bf16[2048,256]{1,0:T(8,128)(2,1)S(1)}, bf16[2048,256]{1,0:T(8,128)(2,1)}, u32[]{:S(2)}) %copy-start.3) | copy-done | bytes 1048600
  24.0 3.6 %critics.1 = f32[8,80,128]{2,1,0:T(8,128)S(1)} custom-call(bf16[2048,256]{1,0:T(8,128)(2,1)S(1)} %copy-done.3, bf16[130,256]{1,0:T(8,128)(2,1)S(1)} %get-tuple-element.22.q0_ref, bf16[130,256]{1,0:T(8,128)(2,1)S(1)} %get-tuple-element.21.q1_ref, bf16[2,256,256]{2,1,0:T(8,128)(2,1)S(1)} %copy-done.4, bf16[2,256]{1,0:T(2,128)(2,1)S(1)} %copy-done.7, ...), custom_call_target="tpu_custom_call" | custom-call | flops 2147483648 | bytes 2000000 | tf_op jit(solution)/shard_map/critics/pallas_call | solution.py:201
  27.6 3.8 %all-to-all-done.1.request_ref = s32[64,1,128]{2,1,0:T(1,128)S(1)} async-done(((s32[64,1,128]{2,1,0:T(1,128)}), s32[64,1,128]{2,1,0:T(1,128)S(1)}, u32[]{:S(2)}, u32[]{:S(2)}) %all-to-all-start.1) | async-done | bytes 32800 | tf_op jit(solution)/shard_map/all_to_all | solution.py:231
  31.4 13.6 %all_to_all.15.tables_ref = f32[8,80,128]{2,1,0:T(8,128)S(1)} all-to-all(f32[8,80,128]{2,1,0:T(8,128)S(1)} %critics.1), channel_id=1, replica_groups=mesh['y'=8,'x'=4,'z'=8,'c'=2] {'x','c'}, dimensions={0} | all-to-all | bytes 655360 | tf_op jit(solution)/shard_map/all_to_all | solution.py:233
  45.0 1.6 %serve.1 = f32[64,8,128]{2,1,0:T(8,128)S(1)} custom-call(f32[8,80,128]{2,1,0:T(8,128)S(1)} %all_to_all.15.tables_ref, s32[64,1,128]{2,1,0:T(1,128)S(1)} %all-to-all-done.1.request_ref), custom_call_target="tpu_custom_call" | custom-call | tf_op jit(solution)/shard_map/serve/pallas_call | solution.py:214
  46.7 0.0 copy-start.1
  46.7 19.8 %all_to_all.16.answer_ref = f32[64,8,128]{2,1,0:T(8,128)S(1)} all-to-all(f32[64,8,128]{2,1,0:T(8,128)S(1)} %serve.1), channel_id=1, replica_groups=mesh['y'=8,'x'=4,'z'=8,'c'=2] {'y','z'}, dimensions={0} | all-to-all | bytes 524288 | tf_op jit(solution)/shard_map/all_to_all | solution.py:235
  66.5 0.0 copy-done.1
  66.5 1.3 %finish.1 = (f32[2,1024]{1,0:T(2,128)}, f32[2,1024]{1,0:T(2,128)}, f32[1,1024]{1,0:T(1,128)}, f32[1,1024]{1,0:T(1,128)}, f32[1,1024]{1,0:T(1,128)}) custom-call(f32[64,8,128]{2,1,0:T(8,128)S(1)} %all_to_all.16.answer_ref, s32[8,128]{1,0:T(8,128)S(1)} %bitcast.10, s32[8,128]{1,0:T(8,128)S(1)} %get-tuple-element.13.rank_ref), custom_call_target="tpu_custom_call" | custom-call | tf_op jit(solution)/shard_map/finish/pallas_call | solution.py:222
  (2 shorter events, 0.0 us)
Async XLA Ops:
  0.6 0.7 %copy-start = (s32[1024,1]{0,1:T(1,128)S(1)}, s32[1024,1]{0,1:T(1,128)}, u32[]{:S(2)}) copy-start(s32[1024,1]{0,1:T(1,128)} %param.10) | copy-start | bytes 12292
  1.3 0.7 %copy-start.2 = (s32[1024]{0:T(1024)S(1)}, s32[1024]{0:T(1024)}, u32[]{:S(2)}) copy-start(s32[1024]{0:T(1024)} %param.11) | copy-start | bytes 12292
  3.4 28.0 %all-to-all-start.1 = ((s32[64,1,128]{2,1,0:T(1,128)}), s32[64,1,128]{2,1,0:T(1,128)S(1)}, u32[]{:S(2)}, u32[]{:S(2)}) async-start(s32[64,1,128]{2,1,0:T(1,128)} %get-tuple-element.12), calls=%async_computation.1 | async-start | bytes 65536 | tf_op jit(solution)/shard_map/all_to_all | solution.py:231
  20.5 1.3 %copy-start.8 = (bf16[256]{0:T(256)(128)(2,1)S(1)}, bf16[256]{0:T(256)(128)(2,1)}, u32[]{:S(2)}) copy-start(bf16[256]{0:T(256)(128)(2,1)} %param.17) | copy-start | bytes 1540
  20.5 1.3 %copy-start.6 = (bf16[124,256]{1,0:T(8,128)(2,1)S(1)}, bf16[124,256]{1,0:T(8,128)(2,1)}, u32[]{:S(2)}) copy-start(bf16[124,256]{1,0:T(8,128)(2,1)} %v_in_ref.1) | copy-start | bytes 190468
  21.8 1.0 %copy-start.4 = (bf16[2,256,256]{2,1,0:T(8,128)(2,1)S(1)}, bf16[2,256,256]{2,1,0:T(8,128)(2,1)}, u32[]{:S(2)}) copy-start(bf16[2,256,256]{2,1,0:T(8,128)(2,1)} %q_mid_ref.1) | copy-start | bytes 786436
  21.8 1.0 %copy-start.5 = (bf16[256,256]{1,0:T(8,128)(2,1)S(1)}, bf16[256,256]{1,0:T(8,128)(2,1)}, u32[]{:S(2)}) copy-start(bf16[256,256]{1,0:T(8,128)(2,1)} %v_mid_ref.1) | copy-start | bytes 393220
  21.9 0.9 %copy-start.7 = (bf16[2,256]{1,0:T(2,128)(2,1)S(1)}, bf16[2,256]{1,0:T(2,128)(2,1)}, u32[]{:S(2)}) copy-start(bf16[2,256]{1,0:T(2,128)(2,1)} %q_out_ref.1) | copy-start | bytes 3076
  22.8 1.2 %copy-start.3 = (bf16[2048,256]{1,0:T(8,128)(2,1)S(1)}, bf16[2048,256]{1,0:T(8,128)(2,1)}, u32[]{:S(2)}) copy-start(bf16[2048,256]{1,0:T(8,128)(2,1)} %rows_ref.1) | copy-start | bytes 3145732
  46.7 19.9 %copy-start.1 = (s32[1024,1]{0,1:T(1,128)S(1)}, s32[1024,1]{0,1:T(1,128)}, u32[]{:S(2)}) copy-start(s32[1024,1]{0,1:T(1,128)} %param.10) | copy-start | bytes 12292

commit v2 on v1

--- a/solution.py
+++ b/solution.py
@@ -36,7 +36,20 @@
     return lax.dot_general(a, b, (((0,), (0,)), ((), ())), preferred_element_type=F32)
 
 
-def request_kernel(owner_ref, local_ref, request_ref, rank_ref):
+def request_kernel(
+    owner_hbm, local_hbm, rows_hbm, q_in_hbm, q_mid_hbm, v_in_hbm, v_mid_hbm,
+    request_ref, rank_ref, rows_ref, q_in_ref, q_mid_ref, v_in_ref, v_mid_ref,
+    owner_ref, local_ref, sems,
+):
+    pairs = (
+        (owner_hbm, owner_ref), (local_hbm, local_ref), (rows_hbm, rows_ref),
+        (q_in_hbm, q_in_ref), (q_mid_hbm, q_mid_ref), (v_in_hbm, v_in_ref), (v_mid_hbm, v_mid_ref),
+    )
+    copies = [pltpu.make_async_copy(a, b, sems.at[i]) for i, (a, b) in enumerate(pairs)]
+    for copy in copies:
+        copy.start()
+    copies[0].wait()
+    copies[1].wait()
     chunks = owner_ref.shape[0]
     owner = owner_ref[...]
     columns = jnp.transpose(owner.astype(F32), (1, 0))
@@ -63,35 +76,38 @@
         low = low + nt(target, jnp.where(place, (local & 127).astype(F32), 0.0).astype(BF16))
     wanted = high.astype(I32) * 128 + low.astype(I32)
     request_ref[...] = wanted.reshape(64, 1, 128)
+    for copy in copies[2:]:
+        copy.wait()
 
 
 def critic_kernel(
-    rows_ref, q0_ref, q1_ref, q_mid_ref, q_out_ref, v_in_ref, v_mid_ref, v_out_ref,
+    rows_ref, q_in_ref, q_mid_ref, v_in_ref, v_mid_ref, q_out_ref, v_out_ref,
     table_ref, first_ref, mid_ref,
 ):
     count, width = rows_ref.shape
     states = v_in_ref.shape[0]
-    pair = q0_ref.shape[0]
-
-    def spread(weights, offset):
+    pair = q_in_ref.shape[0]
+
+    def spread(weights, offset, step=1):
         inner = weights.shape[0]
-        place = jnp.where(iota((inner, width), 1) == iota((inner, width), 0) + offset, 1.0, 0.0)
-        return tn(weights, place.astype(BF16)).astype(BF16)
-
-    first_ref[0:256, :] = spread(q0_ref[...], 0)
-    first_ref[256:512, :] = spread(q1_ref[...], 0)
-    first_ref[512:768, :] = spread(v_in_ref[...], 0)
-    first_ref[768:1024, :] = spread(v_in_ref[...], pair)
-    mid_ref[0] = spread(q_mid_ref[0], 0)
-    mid_ref[1] = spread(q_mid_ref[1], 0)
-    mid_ref[2] = spread(v_mid_ref[...], 0)
-    unit = jnp.where(iota((256, 256), 0) == iota((256, 256), 1), 1.0, 0.0)
-
-    def as_column(row):
-        return jnp.sum(unit * row.astype(F32), axis=1, keepdims=True)
-
-    outs = [as_column(q_out_ref[0:1, :]), as_column(q_out_ref[1:2, :]), as_column(v_out_ref[...])]
-    outs = [jnp.broadcast_to(o, (256, 128)) for o in outs]
+        place = iota((inner, width), 0) == (iota((inner, width), 1) - offset[1]) * step + offset[0]
+        return tn(weights, jnp.where(place, 1.0, 0.0).astype(BF16)).astype(BF16)
+
+    q_both = q_in_ref[...].reshape(2 * pair, width)
+    first_ref[0:256, :] = spread(q_both, (0, 0), 2)
+    first_ref[256:512, :] = spread(q_both, (1, 0), 2)
+    first_ref[512:768, :] = spread(v_in_ref[...], (0, 0))
+    first_ref[768:1024, :] = spread(v_in_ref[...], (0, pair))
+    mid_ref[0] = spread(q_mid_ref[0], (0, 0))
+    mid_ref[1] = spread(q_mid_ref[1], (0, 0))
+    mid_ref[2] = spread(v_mid_ref[...], (0, 0))
+
+    def as_column(row, pick):
+        count = row.shape[0]
+        return tn(row, jnp.where(iota((count, 128), 0) == pick, 1.0, 0.0).astype(BF16))
+
+    q_out = q_out_ref[...]
+    outs = [as_column(q_out, 0), as_column(q_out, 1), as_column(v_out_ref[...], 0)]
     tail = jnp.where(
         iota((8, width), 1) == iota((8, width), 0) + (pair + states), 1.0, 0.0
     ).astype(BF16)
@@ -132,6 +148,7 @@
     high = by_side(wanted >> 7)
     low = by_side(wanted & 127)
     lane_block = iota((8, 128), 1) // SLOTS
+    upper = iota((8, 128), 0) < 4
     for c in range(4):
         high_c = high[:, c * 128 : (c + 1) * 128]
         low_c = low[:, c * 128 : (c + 1) * 128]
@@ -141,31 +158,39 @@
             for v in range(NV):
                 piece = tables_ref[:, v * 16 + k, :]
                 found[v] = jnp.where(here, jnp.take_along_axis(piece, low_c, axis=1), found[v])
-        found = [found[0]] + [pltpu.roll(found[v], v * SLOTS, 1) for v in range(1, NV)]
-        for h in range(16):
-            message = found[0]
-            for v in range(1, NV):
-                message = jnp.where(lane_block == (h + v) % 16, found[v], message)
-            if h:
-                message = pltpu.roll(message, 128 - h * SLOTS, 1)
-            answer_ref[c * 16 + h] = message
+        near = [found[0]] + [pltpu.roll(found[v], v * SLOTS, 1) for v in range(1, NV)]
+        away = [pltpu.roll(pltpu.roll(f, 4, 0), 64, 1) for f in near]
+
+        def message(h, left, right):
+            out = left[0]
+            for v in range(NV):
+                if v:
+                    out = jnp.where(lane_block == (h + v) % 16, left[v], out)
+                out = jnp.where(lane_block == (h + v + 8) % 16, right[v], out)
+            return pltpu.roll(out, 128 - h * SLOTS, 1) if h else out
+
+        for h in range(0, 16, 2):
+            both = jnp.where(upper, message(h, near, away), message((h + 9) % 16, away, near))
+            start = (c * 16 + h) * 4
+            answer_ref[start : start + 8, :] = both
 
 
 def finish_kernel(
     answer_ref, owner_ref, rank_ref, q_ref, values_ref, target_ref, q_loss_ref, value_loss_ref
 ):
-    answers = answer_ref[...].reshape(512, 128)
+    answers = answer_ref[...]
     part_one = answers.astype(BF16)
     rest = answers - part_one.astype(F32)
     part_two = rest.astype(BF16)
     part_three = (rest - part_two.astype(F32)).astype(BF16)
-    parts = [jnp.transpose(p, (1, 0))[: NV * SLOTS, :] for p in (part_one, part_two, part_three)]
+    parts = [jnp.transpose(p, (1, 0)) for p in (part_one, part_two, part_three)]
     for k in range(owner_ref.shape[0]):
         far, side = split_owner(owner_ref[k : k + 1, :])
-        hot = jnp.where(iota((512, 128), 0) == far * 8 + side, 1.0, 0.0).astype(BF16)
+        hot = jnp.where(iota((256, 128), 0) == far * 4 + (side & 3), 1.0, 0.0).astype(BF16)
         got = jnp.dot(parts[0], hot, preferred_element_type=F32)
         got = got + jnp.dot(parts[1], hot, preferred_element_type=F32)
         got = got + jnp.dot(parts[2], hot, preferred_element_type=F32)
+        got = jnp.where(side < 4, got[0:64, :], got[64:128, :])
         mine = iota((8, 128), 0) == rank_ref[k : k + 1, :]
         q0, q1, now, later, target = [
             jnp.sum(
@@ -188,16 +213,24 @@
     return jax.ShapeDtypeStruct(dims, dtype)
 
 
-def make_request(owner, local_row):
+def make_request(owner, local_row, buffer, q_in, q_mid, v_in, v_mid):
+    moved = (buffer, q_in, q_mid, v_in, v_mid)
     return pl.pallas_call(
         request_kernel,
-        out_shape=(shape((64, 1, 128), I32), shape((8, 128), I32)),
+        in_specs=[pl.BlockSpec(memory_space=pl.ANY)] * 7,
+        out_specs=[pl.BlockSpec(memory_space=pltpu.VMEM)] * 7,
+        out_shape=(
+            shape((64, 1, 128), I32), shape((8, 128), I32), *[shape(m.shape, m.dtype) for m in moved]
+        ),
+        scratch_shapes=[
+            pltpu.VMEM((8, 128), I32), pltpu.VMEM((8, 128), I32), pltpu.SemaphoreType.DMA((7,))
+        ],
         compiler_params=SMALL,
         name="make_request",
-    )(owner, local_row)
-
-
-def critics(buffer, q_in, q_mid, q_out, v_in, v_mid, v_out):
+    )(*[pltpu.with_memory_space_constraint(a, pltpu.HBM) for a in (owner, local_row, *moved)])
+
+
+def critics(buffer, q_in, q_mid, v_in, v_mid, q_out, v_out):
     return pl.pallas_call(
         critic_kernel,
         out_shape=shape((8, NV * 16, 128), F32),
@@ -207,12 +240,12 @@
         ),
         compiler_params=SMALL,
         name="critics",
-    )(buffer, q_in[0], q_in[1], q_mid, q_out, v_in, v_mid, v_out.reshape(1, -1))
+    )(buffer, q_in, q_mid, v_in, v_mid, q_out, v_out.reshape(1, -1))
 
 
 def serve(tables, requests):
     return pl.pallas_call(
-        serve_kernel, out_shape=shape((64, 8, 128), F32), compiler_params=SMALL, name="serve"
+        serve_kernel, out_shape=shape((256, 128), F32), compiler_params=SMALL, name="serve"
     )(tables, requests)
 
 
@@ -227,12 +260,13 @@
 def body(buffer, owner, local_row, q_in, q_mid, q_out, v_in, v_mid, v_out):
     owner = owner.reshape(8, 128)
     local_row = local_row.reshape(8, 128)
-    requests, rank = make_request(owner, local_row)
+    q_in = jnp.transpose(q_in, (1, 0, 2))
+    requests, rank, *staged = make_request(owner, local_row, buffer, q_in, q_mid, v_in, v_mid)
     requests = lax.all_to_all(requests, FAR, 0, 0, tiled=True)
-    table = critics(buffer, q_in, q_mid, q_out, v_in, v_mid, v_out)
+    table = critics(*staged, q_out, v_out)
     tables = lax.all_to_all(table, SIDE, 0, 0, tiled=True)
-    answers = serve(tables, requests)
-    answers = lax.all_to_all(answers, FAR, 0, 0, tiled=True)
+    answers = serve(tables, requests).reshape(64, 4, 128)
+    answers = lax.all_to_all(answers, FAR, 0, 0, tiled=True).reshape(256, 128)
     q_values, values, targets, q_loss, value_loss = finish(answers, owner, rank)
     return q_values, values, targets.reshape(-1), q_loss.reshape(-1), value_loss.reshape(-1)
 

time: 69.1 us -> 63.8 us (0.923); the launches traced: 67.8 us -> 63.6 us
  local copies, waits for them, and re-layouts: 4.79 us -> 0.69 us
  blocking collectives: 33.5 us -> 29.8 us
  waiting for transfers between devices: 3.81 us -> 6.43 us
  Pallas kernels: 7.85 us -> 8.79 us
    all_to_all x1, blocking collectives: 19.8 us -> 16.2 us  [body(): answers = lax.all_to_all(answers, FAR, 0, 0, tiled=True).reshape(256, 128)]
    unnamed x18 -> x6, local copies, waits for them, and re-layouts: 3.53 us -> 0.69 us
    all_to_all x1, waiting for transfers between devices: 3.81 us -> 6.43 us  [body(): requests = lax.all_to_all(requests, FAR, 0, 0, tiled=True)]
    slice x1 -> x0, local copies, waits for them, and re-layouts: 1.23 us -> none  [critics(): q_in[1]]
    pallas_call x2, Pallas kernels: 3 us -> 3.85 us  [the longest x1 2.16 us: make_request(): pl.pallas_call(request_kernel, in_specs=[pl.BlockSpec(memory_space=pl.ANY...]
  transfers between devices with their start and end apart: 1 -> 1, of which waited for: 1 -> 1; matrix products, arithmetic and copies ran while one was open for 2% -> 0% of each run, Pallas kernels for 5% -> 6%
where the time goes in v2:
time: 63.8 us; the launch traced here: 63.6 us
  blocking collectives  29.8 us (47%)
  starting transfers between devices  17.1 us (27%)
  Pallas kernels  8.79 us (14%)
  waiting for transfers between devices  6.43 us (10%)
  between operations  0.7 us (1%)
  local copies, waits for them, and re-layouts  0.69 us (1%)
    all_to_all x1, starting transfers between devices, body(): requests = lax.all_to_all(requests, FAR, 0, 0, tiled=True)  17.1 us
    all_to_all x1, blocking collectives, body(): answers = lax.all_to_all(answers, FAR, 0, 0, tiled=True).reshape(256, 128)  16.2 us
    all_to_all x1, blocking collectives, body(): tables = lax.all_to_all(table, SIDE, 0, 0, tiled=True)  13.6 us
    all_to_all x1, waiting for transfers between devices, body(): requests = lax.all_to_all(requests, FAR, 0, 0, tiled=True)  6.43 us
    pallas_call x1, Pallas kernels, critics(): pl.pallas_call(critic_kernel, out_shape=shape((8, NV * 16, 128), F32), sc...  3.71 us
    pallas_call x1, Pallas kernels, make_request(): pl.pallas_call(request_kernel, in_specs=[pl.BlockSpec(memory_space=pl.ANY...  2.16 us
    pallas_call x1, Pallas kernels, serve(): pl.pallas_call(serve_kernel, out_shape=shape((256, 128), F32), compiler_p...  1.69 us
  transfers between devices with their start and end apart: 1, of which 1 were waited for; matrix products, arithmetic and copies ran while one was open for 0% of the time, Pallas kernels for 6%

profile of v2, /device:TPU:1, one launch (start us, length us, event | category | flops | bytes accessed | tf_op | source)
XLA Modules:
  0.0 63.6 jit_solution(12305717989365416898)
XLA Ops:
  0.6 2.2 %make_request.1 = (s32[64,1,128]{2,1,0:T(1,128)}, s32[8,128]{1,0:T(8,128)S(1)}, bf16[2048,256]{1,0:T(8,128)(2,1)S(1)}, bf16[130,2,256]{2,1,0:T(2,128)(2,1)S(1)},...) custom-call(s32[8,128]{1,0:T(8,128)} %bitcast.10, ...), custom_call_target="tpu_custom_call" | custom-call | tf_op jit(solution)/shard_map/make_request/pallas_call | solution.py:218
  2.8 0.0 copy-start.2
  2.8 17.1 %all-to-all-start.1 = ((s32[64,1,128]{2,1,0:T(1,128)}), s32[64,1,128]{2,1,0:T(1,128)S(1)}, u32[]{:S(2)}, u32[]{:S(2)}) async-start(s32[64,1,128]{2,1,0:T(1,128)} %get-tuple-element.22), calls=%async_computation.1 | async-start | bytes 65536 | tf_op jit(solution)/shard_map/all_to_all | solution.py:265
  20.0 0.0 copy-done.2
  20.0 0.0 copy-start.1
  20.0 0.7 %copy-done.1 = bf16[2,256]{1,0:T(2,128)(2,1)S(1)} copy-done((bf16[2,256]{1,0:T(2,128)(2,1)S(1)}, bf16[2,256]{1,0:T(2,128)(2,1)}, u32[]{:S(2)}) %copy-start.1) | copy-done | bytes 1048
  20.7 3.7 %critics.1 = f32[8,80,128]{2,1,0:T(8,128)S(1)} custom-call(bf16[2048,256]{1,0:T(8,128)(2,1)S(1)} %get-tuple-element.17.rows_ref, bf16[130,2,256]{2,1,0:T(2,128)(2,1)S(1)} %get-tuple-element.18.q_in_ref, bf16[2,256,256]{2,1,0:T(8,128)(2,1)S(1)} %get-tuple-element.19.q_mid_ref, bf16[124,256]{1,0:T(8,128)(2,1)S(1)} %get-tuple-element.20.v_in_ref, ...), custom_call_target="tpu_custom_call" | custom-call | flops 2147483648 | bytes 2000000 | tf_op jit(solution)/shard_map/critics/pallas_call | solution.py:234
  24.4 6.4 %all-to-all-done.1.request_ref = s32[64,1,128]{2,1,0:T(1,128)S(1)} async-done(((s32[64,1,128]{2,1,0:T(1,128)}), s32[64,1,128]{2,1,0:T(1,128)S(1)}, u32[]{:S(2)}, u32[]{:S(2)}) %all-to-all-start.1) | async-done | bytes 32800 | tf_op jit(solution)/shard_map/all_to_all | solution.py:265
  30.8 13.6 %all_to_all.15.tables_ref = f32[8,80,128]{2,1,0:T(8,128)S(1)} all-to-all(f32[8,80,128]{2,1,0:T(8,128)S(1)} %critics.1), channel_id=1, replica_groups=mesh['y'=8,'x'=4,'z'=8,'c'=2] {'x','c'}, dimensions={0} | all-to-all | bytes 655360 | tf_op jit(solution)/shard_map/all_to_all | solution.py:267
  44.5 1.7 %serve.1 = f32[256,128]{1,0:T(8,128)S(1)} custom-call(f32[8,80,128]{2,1,0:T(8,128)S(1)} %all_to_all.15.tables_ref, s32[64,1,128]{2,1,0:T(1,128)S(1)} %all-to-all-done.1.request_ref), custom_call_target="tpu_custom_call" | custom-call | tf_op jit(solution)/shard_map/serve/pallas_call | solution.py:247
  46.1 0.0 copy-start
  46.2 16.2 %all_to_all.16 = f32[64,4,128]{2,1,0:T(4,128)S(1)} all-to-all(f32[64,4,128]{2,1,0:T(4,128)S(1)} %bitcast.9), channel_id=1, replica_groups=mesh['y'=8,'x'=4,'z'=8,'c'=2] {'y','z'}, dimensions={0} | all-to-all | bytes 262144 | tf_op jit(solution)/shard_map/all_to_all | solution.py:269
  62.4 0.0 copy-done
  62.4 1.2 %finish.1 = (f32[2,1024]{1,0:T(2,128)}, f32[2,1024]{1,0:T(2,128)}, f32[1,1024]{1,0:T(1,128)}, f32[1,1024]{1,0:T(1,128)}, f32[1,1024]{1,0:T(1,128)}) custom-call(f32[256,128]{1,0:T(8,128)S(1)} %bitcast.8, s32[8,128]{1,0:T(8,128)S(1)} %bitcast.11, s32[8,128]{1,0:T(8,128)S(1)} %get-tuple-element.23.rank_ref), custom_call_target="tpu_custom_call" | custom-call | tf_op jit(solution)/shard_map/finish/pallas_call | solution.py:255
  (1 shorter events, 0.0 us)
Async XLA Ops:
  2.8 17.2 %copy-start.2 = (bf16[256]{0:T(256)(128)(2,1)S(1)}, bf16[256]{0:T(256)(128)(2,1)}, u32[]{:S(2)}) copy-start(bf16[256]{0:T(256)(128)(2,1)} %param.17) | copy-start | bytes 1540
  2.8 28.0 %all-to-all-start.1 = ((s32[64,1,128]{2,1,0:T(1,128)}), s32[64,1,128]{2,1,0:T(1,128)S(1)}, u32[]{:S(2)}, u32[]{:S(2)}) async-start(s32[64,1,128]{2,1,0:T(1,128)} %get-tuple-element.22), calls=%async_computation.1 | async-start | bytes 65536 | tf_op jit(solution)/shard_map/all_to_all | solution.py:265
  20.0 0.7 %copy-start.1 = (bf16[2,256]{1,0:T(2,128)(2,1)S(1)}, bf16[2,256]{1,0:T(2,128)(2,1)}, u32[]{:S(2)}) copy-start(bf16[2,256]{1,0:T(2,128)(2,1)} %q_out_ref.1) | copy-start | bytes 3076
  46.1 16.2 %copy-start = (s32[1024,1]{0,1:T(1,128)S(1)}, s32[1024,1]{0,1:T(1,128)}, u32[]{:S(2)}) copy-start(s32[1024,1]{0,1:T(1,128)} %param.10) | copy-start | bytes 12292

commit v3 on v2

--- a/solution.py
+++ b/solution.py
@@ -7,6 +7,9 @@
 from jax.sharding import PartitionSpec as P
 
 FAR = ("y", "z")
+ASK = 37
+REPLY = 36
+SHARE = 5
 SIDE = ("x", "c")
 SLOTS = 8
 NV = 5
@@ -21,7 +24,11 @@
     x = (owner >> 4) & 3
     z = (owner >> 1) & 7
     c = owner & 1
-    return y * 8 + z, x * 2 + c
+    return y * 8 + z, (x * 2 + c) ^ SHARE
+
+
+def listed(count, first):
+    return [[i ^ first for i in range(count)]]
 
 
 def iota(shape, dim):
@@ -37,13 +44,14 @@
 
 
 def request_kernel(
-    owner_hbm, local_hbm, rows_hbm, q_in_hbm, q_mid_hbm, v_in_hbm, v_mid_hbm,
-    request_ref, rank_ref, rows_ref, q_in_ref, q_mid_ref, v_in_ref, v_mid_ref,
-    owner_ref, local_ref, sems,
+    owner_hbm, local_hbm, rows_hbm, q_in_hbm, q_mid_hbm, v_in_hbm, v_mid_hbm, q_out_hbm, v_out_hbm,
+    request_ref, rank_ref, rows_ref, q_in_ref, q_mid_ref, v_in_ref, v_mid_ref, q_out_ref, v_out_ref,
+    owner_ref, local_ref, target_ref, value_ref, sems,
 ):
     pairs = (
         (owner_hbm, owner_ref), (local_hbm, local_ref), (rows_hbm, rows_ref),
         (q_in_hbm, q_in_ref), (q_mid_hbm, q_mid_ref), (v_in_hbm, v_in_ref), (v_mid_hbm, v_mid_ref),
+        (q_out_hbm, q_out_ref), (v_out_hbm, v_out_ref),
     )
     copies = [pltpu.make_async_copy(a, b, sems.at[i]) for i, (a, b) in enumerate(pairs)]
     for copy in copies:
@@ -63,18 +71,18 @@
             if k == q:
                 same = jnp.logical_and(same, before)
             totals[k] = totals[k] + jnp.where(same, 1.0, 0.0)
-    high = jnp.zeros((64, 128), F32)
-    low = jnp.zeros((64, 128), F32)
     for k in range(chunks):
+        span = slice(k * 128, (k + 1) * 128)
         rank = jnp.sum(totals[k], axis=0, keepdims=True).astype(I32)
         rank_ref[k : k + 1, :] = rank
         far, side = split_owner(owner_ref[k : k + 1, :])
         local = local_ref[k : k + 1, :]
-        place = iota((128, 128), 0) == side * SLOTS + rank
-        target = jnp.where(iota((64, 128), 0) == far, 1.0, 0.0).astype(BF16)
-        high = high + nt(target, jnp.where(place, (local >> 7).astype(F32), 0.0).astype(BF16))
-        low = low + nt(target, jnp.where(place, (local & 127).astype(F32), 0.0).astype(BF16))
-    wanted = high.astype(I32) * 128 + low.astype(I32)
+        place = iota((64, 128), 0) == side * SLOTS + rank
+        target_ref[:, span] = jnp.where(iota((64, 128), 0) == far ^ ASK, 1.0, 0.0).astype(BF16)
+        value_ref[0:64, span] = jnp.where(place, (local >> 7).astype(F32), 0.0).astype(BF16)
+        value_ref[64:128, span] = jnp.where(place, (local & 127).astype(F32), 0.0).astype(BF16)
+    both = nt(target_ref[...], value_ref[...]).astype(I32)
+    wanted = both * 128 + pltpu.roll(both, 64, 1)
     request_ref[...] = wanted.reshape(64, 1, 128)
     for copy in copies[2:]:
         copy.wait()
@@ -107,7 +115,7 @@
         return tn(row, jnp.where(iota((count, 128), 0) == pick, 1.0, 0.0).astype(BF16))
 
     q_out = q_out_ref[...]
-    outs = [as_column(q_out, 0), as_column(q_out, 1), as_column(v_out_ref[...], 0)]
+    outs = [as_column(q_out, 0), as_column(q_out, 1), as_column(v_out_ref[...].reshape(1, 256), 0)]
     tail = jnp.where(
         iota((8, width), 1) == iota((8, width), 0) + (pair + states), 1.0, 0.0
     ).astype(BF16)
@@ -135,29 +143,32 @@
                     table_ref[s, row : row + 1, :] = piece
 
 
-def serve_kernel(tables_ref, request_ref, answer_ref):
-    wanted = request_ref[...].reshape(64, 128)
-    expand = jnp.where(iota((64, 512), 0) == iota((64, 512), 1) // SLOTS, 1.0, 0.0).astype(BF16)
-    own = iota((128, 512), 0) % SLOTS == iota((128, 512), 1) % SLOTS
-    gather_side = jnp.where(iota((8, 128), 0) == iota((8, 128), 1) // SLOTS, 1.0, 0.0).astype(BF16)
-
-    def by_side(values):
-        wide = jnp.where(own, tn(values.astype(F32).astype(BF16), expand), 0.0).astype(BF16)
-        return jnp.dot(gather_side, wide, preferred_element_type=F32).astype(I32)
-
-    high = by_side(wanted >> 7)
-    low = by_side(wanted & 127)
-    lane_block = iota((8, 128), 1) // SLOTS
+def serve_kernel(tables_ref, request_ref, answer_ref, turned_ref):
+    turned_ref[...] = jnp.transpose(request_ref[...].reshape(64, 128).astype(F32), (1, 0))
+    lane = iota((8, 128), 1)
+    lane_block = lane // SLOTS
     upper = iota((8, 128), 0) < 4
+    wanted = [jnp.zeros((8, 128), F32) for _ in range(4)]
+    for s in range(SLOTS):
+        rows = turned_ref[pl.ds(s, 8, stride=SLOTS), :]
+        if rows.shape[1] < 128:
+            rows = jnp.concatenate([rows, rows], axis=1)
+        for c in range(4):
+            spread = jnp.take_along_axis(rows, lane_block + c * 16, axis=1)
+            wanted[c] = jnp.where(lane % SLOTS == s, spread, wanted[c])
+    wanted = [w.astype(I32) for w in wanted]
+    low = [w & 127 for w in wanted]
+    high = [w >> 7 for w in wanted]
+    looked_up = [[jnp.zeros((8, 128), F32) for _ in range(NV)] for _ in range(4)]
+    for k in range(16):
+        here = [h == k for h in high]
+        for v in range(NV):
+            piece = tables_ref[:, v * 16 + k, :]
+            for c in range(4):
+                got = jnp.take_along_axis(piece, low[c], axis=1)
+                looked_up[c][v] = jnp.where(here[c], got, looked_up[c][v])
     for c in range(4):
-        high_c = high[:, c * 128 : (c + 1) * 128]
-        low_c = low[:, c * 128 : (c + 1) * 128]
-        found = [jnp.zeros((8, 128), F32) for _ in range(NV)]
-        for k in range(16):
-            here = high_c == k
-            for v in range(NV):
-                piece = tables_ref[:, v * 16 + k, :]
-                found[v] = jnp.where(here, jnp.take_along_axis(piece, low_c, axis=1), found[v])
+        found = looked_up[c]
         near = [found[0]] + [pltpu.roll(found[v], v * SLOTS, 1) for v in range(1, NV)]
         away = [pltpu.roll(pltpu.roll(f, 4, 0), 64, 1) for f in near]
 
@@ -170,7 +181,8 @@
             return pltpu.roll(out, 128 - h * SLOTS, 1) if h else out
 
         for h in range(0, 16, 2):
-            both = jnp.where(upper, message(h, near, away), message((h + 9) % 16, away, near))
+            one, two = h ^ ASK ^ REPLY, (h + 1) ^ ASK ^ REPLY
+            both = jnp.where(upper, message(one, near, away), message((two + 8) % 16, away, near))
             start = (c * 16 + h) * 4
             answer_ref[start : start + 8, :] = both
 
@@ -186,7 +198,7 @@
     parts = [jnp.transpose(p, (1, 0)) for p in (part_one, part_two, part_three)]
     for k in range(owner_ref.shape[0]):
         far, side = split_owner(owner_ref[k : k + 1, :])
-        hot = jnp.where(iota((256, 128), 0) == far * 4 + (side & 3), 1.0, 0.0).astype(BF16)
+        hot = jnp.where(iota((256, 128), 0) == (far ^ REPLY) * 4 + (side & 3), 1.0, 0.0).astype(BF16)
         got = jnp.dot(parts[0], hot, preferred_element_type=F32)
         got = got + jnp.dot(parts[1], hot, preferred_element_type=F32)
         got = got + jnp.dot(parts[2], hot, preferred_element_type=F32)
@@ -213,17 +225,17 @@
     return jax.ShapeDtypeStruct(dims, dtype)
 
 
-def make_request(owner, local_row, buffer, q_in, q_mid, v_in, v_mid):
-    moved = (buffer, q_in, q_mid, v_in, v_mid)
+def make_request(owner, local_row, *moved):
     return pl.pallas_call(
         request_kernel,
-        in_specs=[pl.BlockSpec(memory_space=pl.ANY)] * 7,
-        out_specs=[pl.BlockSpec(memory_space=pltpu.VMEM)] * 7,
+        in_specs=[pl.BlockSpec(memory_space=pl.ANY)] * (2 + len(moved)),
+        out_specs=[pl.BlockSpec(memory_space=pltpu.VMEM)] * (2 + len(moved)),
         out_shape=(
             shape((64, 1, 128), I32), shape((8, 128), I32), *[shape(m.shape, m.dtype) for m in moved]
         ),
         scratch_shapes=[
-            pltpu.VMEM((8, 128), I32), pltpu.VMEM((8, 128), I32), pltpu.SemaphoreType.DMA((7,))
+            pltpu.VMEM((8, 128), I32), pltpu.VMEM((8, 128), I32),
+            pltpu.VMEM((64, 1024), BF16), pltpu.VMEM((128, 1024), BF16), pltpu.SemaphoreType.DMA((2 + len(moved),))
         ],
         compiler_params=SMALL,
         name="make_request",
@@ -240,12 +252,13 @@
         ),
         compiler_params=SMALL,
         name="critics",
-    )(buffer, q_in, q_mid, v_in, v_mid, q_out, v_out.reshape(1, -1))
+    )(buffer, q_in, q_mid, v_in, v_mid, q_out, v_out)
 
 
 def serve(tables, requests):
     return pl.pallas_call(
-        serve_kernel, out_shape=shape((256, 128), F32), compiler_params=SMALL, name="serve"
+        serve_kernel, out_shape=shape((256, 128), F32), scratch_shapes=[pltpu.VMEM((128, 64), F32)],
+        compiler_params=SMALL, name="serve",
     )(tables, requests)
 
 
@@ -261,12 +274,14 @@
     owner = owner.reshape(8, 128)
     local_row = local_row.reshape(8, 128)
     q_in = jnp.transpose(q_in, (1, 0, 2))
-    requests, rank, *staged = make_request(owner, local_row, buffer, q_in, q_mid, v_in, v_mid)
-    requests = lax.all_to_all(requests, FAR, 0, 0, tiled=True)
-    table = critics(*staged, q_out, v_out)
-    tables = lax.all_to_all(table, SIDE, 0, 0, tiled=True)
+    requests, rank, *staged = make_request(
+        owner, local_row, buffer, q_in, q_mid, v_in, v_mid, q_out, v_out
+    )
+    requests = lax.all_to_all(requests, FAR, 0, 0, axis_index_groups=listed(64, ASK), tiled=True)
+    table = critics(*staged)
+    tables = lax.all_to_all(table, SIDE, 0, 0, axis_index_groups=listed(8, SHARE), tiled=True)
     answers = serve(tables, requests).reshape(64, 4, 128)
-    answers = lax.all_to_all(answers, FAR, 0, 0, tiled=True).reshape(256, 128)
+    answers = lax.all_to_all(answers, FAR, 0, 0, axis_index_groups=listed(64, REPLY), tiled=True).reshape(256, 128)
     q_values, values, targets, q_loss, value_loss = finish(answers, owner, rank)
     return q_values, values, targets.reshape(-1), q_loss.reshape(-1), value_loss.reshape(-1)
 

time: 63.8 us -> 55.3 us (0.87)
  waiting for transfers between devices: 6.43 us -> 0.01 us
  blocking collectives: 29.8 us -> 26.4 us
  starting transfers between devices: 17.1 us -> 19.2 us
  local copies, waits for them, and re-layouts: 0.69 us -> 0.01 us
    all_to_all x1, waiting for transfers between devices: 6.43 us -> 0.01 us  [body(): lax.all_to_all(requests, FAR, 0, 0, axis_index_groups=listed(64, ASK), ti...]
    all_to_all x2, blocking collectives: 29.8 us -> 26.4 us  [the longest x1 15.4 us: body(): lax.all_to_all(answers, FAR, 0, 0, axis_index_groups=listed(64, REPLY), t...]
    all_to_all x1, starting transfers between devices: 17.1 us -> 19.2 us  [body(): lax.all_to_all(requests, FAR, 0, 0, axis_index_groups=listed(64, ASK), ti...]
    unnamed x6 -> x2, local copies, waits for them, and re-layouts: 0.69 us -> 0.01 us
  transfers between devices with their start and end apart: 1 -> 1, of which waited for: 1 -> 0; matrix products, arithmetic and copies ran while one was open for 0% -> 0% of each run, Pallas kernels for 6% -> 7%
where the time goes in v3:
time: 55.3 us; the launch traced here: 55.1 us
  blocking collectives  26.4 us (48%)
  starting transfers between devices  19.2 us (35%)
  Pallas kernels  8.74 us (16%)
  between operations  0.68 us (1%)
    all_to_all x1, starting transfers between devices, body(): lax.all_to_all(requests, FAR, 0, 0, axis_index_groups=listed(64, ASK), ti...  19.2 us
    all_to_all x1, blocking collectives, body(): lax.all_to_all(answers, FAR, 0, 0, axis_index_groups=listed(64, REPLY), t...  15.4 us
    all_to_all x1, blocking collectives, body(): lax.all_to_all(table, SIDE, 0, 0, axis_index_groups=listed(8, SHARE), til...  11 us
    pallas_call x1, Pallas kernels, critics(): pl.pallas_call(critic_kernel, out_shape=shape((8, NV * 16, 128), F32), sc...  3.71 us
    pallas_call x1, Pallas kernels, make_request(): pl.pallas_call(request_kernel, in_specs=[pl.BlockSpec(memory_space=pl.ANY...  2.16 us
    pallas_call x1, Pallas kernels, serve(): pl.pallas_call(serve_kernel, out_shape=shape((256, 128), F32), scratch_sh...  1.64 us
    pallas_call x1, Pallas kernels, finish(): pl.pallas_call(finish_kernel, out_shape=(two, two, line, line, line), com...  1.23 us
  transfers between devices with their start and end apart: 1, of which 0 were waited for; matrix products, arithmetic and copies ran while one was open for 0% of the time, Pallas kernels for 7%

profile of v3, /device:TPU:1, one launch (start us, length us, event | category | flops | bytes accessed | tf_op | source)
XLA Modules:
  0.0 55.1 jit_solution(14747280563552276669)
XLA Ops:
  0.6 2.2 %make_request.1 = (s32[64,1,128]{2,1,0:T(1,128)}, s32[8,128]{1,0:T(8,128)S(1)}, bf16[2048,256]{1,0:T(8,128)(2,1)S(1)}, bf16[130,2,256]{2,1,0:T(2,128)(2,1)S(1)},...) custom-call(s32[8,128]{1,0:T(8,128)} %bitcast.10, ...), custom_call_target="tpu_custom_call" | custom-call | tf_op jit(solution)/shard_map/make_request/pallas_call | solution.py:229
  2.8 19.2 %all-to-all-start.1 = ((s32[64,1,128]{2,1,0:T(1,128)}), s32[64,1,128]{2,1,0:T(1,128)S(1)}, u32[]{:S(2)}, u32[]{:S(2)}) async-start(s32[64,1,128]{2,1,0:T(1,128)} %get-tuple-element.26), calls=%async_computation.1 | async-start | bytes 65536 | tf_op jit(solution)/shard_map/all_to_all | solution.py:280
  22.1 3.7 %critics.1 = f32[8,80,128]{2,1,0:T(8,128)S(1)} custom-call(bf16[2048,256]{1,0:T(8,128)(2,1)S(1)} %get-tuple-element.19.rows_ref, bf16[130,2,256]{2,1,0:T(2,128)(2,1)S(1)} %get-tuple-element.20.q_in_ref, bf16[2,256,256]{2,1,0:T(8,128)(2,1)S(1)} %get-tuple-element.21.q_mid_ref, bf16[124,256]{1,0:T(8,128)(2,1)S(1)} %get-tuple-element.22.v_in_ref, ...), custom_call_target="tpu_custom_call" | custom-call | flops 2147483648 | bytes 2000000 | tf_op jit(solution)/shard_map/critics/pallas_call | solution.py:246
  25.8 0.0 all-to-all-done.1.request_ref
  25.8 11.0 %all_to_all.15.tables_ref = f32[8,80,128]{2,1,0:T(8,128)S(1)} all-to-all(f32[8,80,128]{2,1,0:T(8,128)S(1)} %critics.1), channel_id=1, replica_groups={{33,32,49,48,1,0,17,16},{35,34,51,50,3,2,19,18},{37,36,53,52,5,4,21,20}..., dimensions={0} | all-to-all | bytes 655360 | tf_op jit(solution)/shard_map/all_to_all | solution.py:282
  36.8 1.6 %serve.1 = f32[256,128]{1,0:T(8,128)S(1)} custom-call(f32[8,80,128]{2,1,0:T(8,128)S(1)} %all_to_all.15.tables_ref, s32[64,1,128]{2,1,0:T(1,128)S(1)} %all-to-all-done.1.request_ref), custom_call_target="tpu_custom_call" | custom-call | tf_op jit(solution)/shard_map/serve/pallas_call | solution.py:259
  38.4 0.0 copy-start
  38.4 15.4 %all_to_all.16 = f32[64,4,128]{2,1,0:T(4,128)S(1)} all-to-all(f32[64,4,128]{2,1,0:T(4,128)S(1)} %bitcast.9), channel_id=1, replica_groups={{264,266,268,270,256,258,260,262,328,330,332,334,320,322,324,326,392,39..., dimensions={0} | all-to-all | bytes 262144 | tf_op jit(solution)/shard_map/all_to_all | solution.py:284
  53.8 0.0 copy-done
  53.8 1.2 %finish.1 = (f32[2,1024]{1,0:T(2,128)}, f32[2,1024]{1,0:T(2,128)}, f32[1,1024]{1,0:T(1,128)}, f32[1,1024]{1,0:T(1,128)}, f32[1,1024]{1,0:T(1,128)}) custom-call(f32[256,128]{1,0:T(8,128)S(1)} %bitcast.8, s32[8,128]{1,0:T(8,128)S(1)} %bitcast.11, s32[8,128]{1,0:T(8,128)S(1)} %get-tuple-element.27.rank_ref), custom_call_target="tpu_custom_call" | custom-call | tf_op jit(solution)/shard_map/finish/pallas_call | solution.py:268
Async XLA Ops:
  2.8 23.0 %all-to-all-start.1 = ((s32[64,1,128]{2,1,0:T(1,128)}), s32[64,1,128]{2,1,0:T(1,128)S(1)}, u32[]{:S(2)}, u32[]{:S(2)}) async-start(s32[64,1,128]{2,1,0:T(1,128)} %get-tuple-element.26), calls=%async_computation.1 | async-start | bytes 65536 | tf_op jit(solution)/shard_map/all_to_all | solution.py:280
  38.4 15.4 %copy-start = (s32[1024,1]{0,1:T(1,128)S(1)}, s32[1024,1]{0,1:T(1,128)}, u32[]{:S(2)}) copy-start(s32[1024,1]{0,1:T(1,128)} %param.10) | copy-start | bytes 12292

commit v4 on v3

--- a/solution.py
+++ b/solution.py
@@ -12,7 +12,7 @@
 SHARE = 5
 SIDE = ("x", "c")
 SLOTS = 8
-NV = 5
+NV = 7
 F32 = jnp.float32
 BF16 = jnp.bfloat16
 I32 = jnp.int32
@@ -90,7 +90,7 @@
 
 def critic_kernel(
     rows_ref, q_in_ref, q_mid_ref, v_in_ref, v_mid_ref, q_out_ref, v_out_ref,
-    table_ref, first_ref, mid_ref,
+    table_ref, first_ref, mid_ref, lines_ref,
 ):
     count, width = rows_ref.shape
     states = v_in_ref.shape[0]
@@ -133,17 +133,23 @@
             hidden = jnp.maximum(hidden, 0.0)
             weight = jnp.concatenate([outs[m]] * (block // 128), axis=1)
             results.append(jnp.sum(hidden * weight, axis=0, keepdims=True))
-        target = ends[0:1, :] + ends[1:2, :] * results[3]
-        results.append(target)
-        for v in range(NV):
+        q0, q1, now, later = results
+        target = ends[0:1, :] + ends[1:2, :] * later
+        q_loss = (q0 - target) ** 2 + (q1 - target) ** 2
+        gap = jnp.minimum(q0, q1) - now
+        value_loss = jnp.where(gap < 0.0, 0.3, 0.7) * gap * gap
+        for v, result in enumerate((q0, q1, now, later, target, q_loss, value_loss)):
             for half in range(block // 128):
                 row = v * 16 + b * (block // 128) + half
-                piece = results[v][:, half * 128 : (half + 1) * 128]
-                for s in range(8):
-                    table_ref[s, row : row + 1, :] = piece
-
-
-def serve_kernel(tables_ref, request_ref, answer_ref, turned_ref):
+                lines_ref[row : row + 1, :] = result[:, half * 128 : (half + 1) * 128]
+    table = lines_ref[...].astype(BF16)
+    for s in range(8):
+        table_ref[s] = table
+
+
+def serve_kernel(packed_ref, request_ref, answer_ref, turned_ref, tables_ref):
+    for s in range(8):
+        tables_ref[s] = packed_ref[s].astype(F32)
     turned_ref[...] = jnp.transpose(request_ref[...].reshape(64, 128).astype(F32), (1, 0))
     lane = iota((8, 128), 1)
     lane_block = lane // SLOTS
@@ -184,27 +190,20 @@
             one, two = h ^ ASK ^ REPLY, (h + 1) ^ ASK ^ REPLY
             both = jnp.where(upper, message(one, near, away), message((two + 8) % 16, away, near))
             start = (c * 16 + h) * 4
-            answer_ref[start : start + 8, :] = both
+            answer_ref[start : start + 8, :] = both.astype(BF16)
 
 
 def finish_kernel(
     answer_ref, owner_ref, rank_ref, q_ref, values_ref, target_ref, q_loss_ref, value_loss_ref
 ):
-    answers = answer_ref[...]
-    part_one = answers.astype(BF16)
-    rest = answers - part_one.astype(F32)
-    part_two = rest.astype(BF16)
-    part_three = (rest - part_two.astype(F32)).astype(BF16)
-    parts = [jnp.transpose(p, (1, 0)) for p in (part_one, part_two, part_three)]
+    answers = jnp.transpose(answer_ref[...], (1, 0))
     for k in range(owner_ref.shape[0]):
         far, side = split_owner(owner_ref[k : k + 1, :])
         hot = jnp.where(iota((256, 128), 0) == (far ^ REPLY) * 4 + (side & 3), 1.0, 0.0).astype(BF16)
-        got = jnp.dot(parts[0], hot, preferred_element_type=F32)
-        got = got + jnp.dot(parts[1], hot, preferred_element_type=F32)
-        got = got + jnp.dot(parts[2], hot, preferred_element_type=F32)
+        got = jnp.dot(answers, hot, preferred_element_type=F32)
         got = jnp.where(side < 4, got[0:64, :], got[64:128, :])
         mine = iota((8, 128), 0) == rank_ref[k : k + 1, :]
-        q0, q1, now, later, target = [
+        q0, q1, now, later, target, q_loss, value_loss = [
             jnp.sum(
                 jnp.where(mine, got[v * SLOTS : (v + 1) * SLOTS, :], 0.0), axis=0, keepdims=True
             )
@@ -216,9 +215,8 @@
         values_ref[0:1, span] = now
         values_ref[1:2, span] = later
         target_ref[:, span] = target
-        q_loss_ref[:, span] = (q0 - target) ** 2 + (q1 - target) ** 2
-        gap = jnp.minimum(q0, q1) - now
-        value_loss_ref[:, span] = jnp.where(gap < 0.0, 0.3, 0.7) * gap * gap
+        q_loss_ref[:, span] = q_loss
+        value_loss_ref[:, span] = value_loss
 
 
 def shape(dims, dtype):
@@ -245,8 +243,10 @@
 def critics(buffer, q_in, q_mid, v_in, v_mid, q_out, v_out):
     return pl.pallas_call(
         critic_kernel,
-        out_shape=shape((8, NV * 16, 128), F32),
-        scratch_shapes=[pltpu.VMEM((1024, 256), BF16), pltpu.VMEM((3, 256, 256), BF16)],
+        out_shape=shape((8, NV * 16, 128), BF16),
+        scratch_shapes=[
+            pltpu.VMEM((1024, 256), BF16), pltpu.VMEM((3, 256, 256), BF16), pltpu.VMEM((NV * 16, 128), F32)
+        ],
         cost_estimate=pl.CostEstimate(
             flops=2 * 2048 * 1024 * 512, bytes_accessed=2_000_000, transcendentals=0
         ),
@@ -257,7 +257,8 @@
 
 def serve(tables, requests):
     return pl.pallas_call(
-        serve_kernel, out_shape=shape((256, 128), F32), scratch_shapes=[pltpu.VMEM((128, 64), F32)],
+        serve_kernel, out_shape=shape((256, 128), BF16),
+        scratch_shapes=[pltpu.VMEM((128, 64), F32), pltpu.VMEM((8, NV * 16, 128), F32)],
         compiler_params=SMALL, name="serve",
     )(tables, requests)
 

time: 55.3 us -> 52.4 us (0.948)
  blocking collectives: 26.4 us -> 23.8 us
    all_to_all x1, blocking collectives: 15.4 us -> 14 us  [body(): lax.all_to_all(answers, FAR, 0, 0, axis_index_groups=listed(64, REPLY), t...]
    all_to_all x1, blocking collectives: 11 us -> 9.76 us  [body(): lax.all_to_all(table, SIDE, 0, 0, axis_index_groups=listed(8, SHARE), til...]
where the time goes in v4:
time: 52.4 us; the launch traced here: 51.9 us
  blocking collectives  23.8 us (45%)
  starting transfers between devices  19.2 us (37%)
  Pallas kernels  8.19 us (16%)
  between operations  0.68 us (1%)
    all_to_all x1, starting transfers between devices, body(): lax.all_to_all(requests, FAR, 0, 0, axis_index_groups=listed(64, ASK), ti...  19.2 us
    all_to_all x1, blocking collectives, body(): lax.all_to_all(answers, FAR, 0, 0, axis_index_groups=listed(64, REPLY), t...  14 us
    all_to_all x1, blocking collectives, body(): lax.all_to_all(table, SIDE, 0, 0, axis_index_groups=listed(8, SHARE), til...  9.76 us
    pallas_call x1, Pallas kernels, critics(): pl.pallas_call(critic_kernel, out_shape=shape((8, NV * 16, 128), BF16), s...  3.72 us
    pallas_call x1, Pallas kernels, make_request(): pl.pallas_call(request_kernel, in_specs=[pl.BlockSpec(memory_space=pl.ANY...  2.16 us
    pallas_call x1, Pallas kernels, serve(): pl.pallas_call(serve_kernel, out_shape=shape((256, 128), BF16), scratch_s...  1.38 us
  transfers between devices with their start and end apart: 1, of which 0 were waited for; matrix products, arithmetic and copies ran while one was open for 0% of the time, Pallas kernels for 7%

profile of v4, /device:TPU:1, one launch (start us, length us, event | category | flops | bytes accessed | tf_op | source)
XLA Modules:
  0.0 51.9 jit_solution(8972876984126598503)
XLA Ops:
  0.6 2.2 %make_request.1 = (s32[64,1,128]{2,1,0:T(1,128)}, s32[8,128]{1,0:T(8,128)S(1)}, bf16[2048,256]{1,0:T(8,128)(2,1)S(1)}, bf16[130,2,256]{2,1,0:T(2,128)(2,1)S(1)},...) custom-call(s32[8,128]{1,0:T(8,128)} %bitcast.10, ...), custom_call_target="tpu_custom_call" | custom-call | tf_op jit(solution)/shard_map/make_request/pallas_call | solution.py:227
  2.8 19.2 %all-to-all-start.1 = ((s32[64,1,128]{2,1,0:T(1,128)}), s32[64,1,128]{2,1,0:T(1,128)S(1)}, u32[]{:S(2)}, u32[]{:S(2)}) async-start(s32[64,1,128]{2,1,0:T(1,128)} %get-tuple-element.26), calls=%async_computation.1 | async-start | bytes 65536 | tf_op jit(solution)/shard_map/all_to_all | solution.py:281
  22.1 3.7 %critics.1 = bf16[8,112,128]{2,1,0:T(8,128)(2,1)S(1)} custom-call(bf16[2048,256]{1,0:T(8,128)(2,1)S(1)} %get-tuple-element.19.rows_ref, bf16[130,2,256]{2,1,0:T(2,128)(2,1)S(1)} %get-tuple-element.20.q_in_ref, bf16[2,256,256]{2,1,0:T(8,128)(2,1)S(1)} %get-tuple-element.21.q_mid_ref, bf16[124,256]{1,0:T(8,128)(2,1)S(1)} %get-tuple-element.22.v_in_ref, ...), custom_call_target="tpu_custom_call" | custom-call | flops 2147483648 | bytes 2000000 | tf_op jit(solution)/shard_map/critics/pallas_call | solution.py:244
  25.8 0.0 all-to-all-done.1.request_ref
  25.8 9.8 %all_to_all.15.packed_ref = bf16[8,112,128]{2,1,0:T(8,128)(2,1)S(1)} all-to-all(bf16[8,112,128]{2,1,0:T(8,128)(2,1)S(1)} %critics.1), channel_id=1, replica_groups={{33,32,49,48,1,0,17,16},{35,34,51,50,3,2,19,18},{37,36,53,52,5,4,21,20}..., dimensions={0} | all-to-all | bytes 458752 | tf_op jit(solution)/shard_map/all_to_all | solution.py:283
  35.5 1.4 %serve.1 = bf16[256,128]{1,0:T(8,128)(2,1)S(1)} custom-call(bf16[8,112,128]{2,1,0:T(8,128)(2,1)S(1)} %all_to_all.15.packed_ref, s32[64,1,128]{2,1,0:T(1,128)S(1)} %all-to-all-done.1.request_ref), custom_call_target="tpu_custom_call" | custom-call | tf_op jit(solution)/shard_map/serve/pallas_call | solution.py:259
  36.9 0.0 copy-start
  36.9 14.0 %all_to_all.16 = bf16[64,4,128]{2,1,0:T(4,128)(2,1)S(1)} all-to-all(bf16[64,4,128]{2,1,0:T(4,128)(2,1)S(1)} %bitcast.8), channel_id=1, replica_groups={{264,266,268,270,256,258,260,262,328,330,332,334,320,322,324,326,392,39..., dimensions={0} | all-to-all | bytes 131072 | tf_op jit(solution)/shard_map/all_to_all | solution.py:285
  51.0 0.0 copy-done
  51.0 0.9 %finish.1 = (f32[2,1024]{1,0:T(2,128)}, f32[2,1024]{1,0:T(2,128)}, f32[1,1024]{1,0:T(1,128)}, f32[1,1024]{1,0:T(1,128)}, f32[1,1024]{1,0:T(1,128)}) custom-call(bf16[256,128]{1,0:T(8,128)(2,1)S(1)} %bitcast.9, s32[8,128]{1,0:T(8,128)S(1)} %bitcast.11, s32[8,128]{1,0:T(8,128)S(1)} %get-tuple-element.27.rank_ref), custom_call_target="tpu_custom_call" | custom-call | tf_op jit(solution)/shard_map/finish/pallas_call | solution.py:269
Async XLA Ops:
  2.8 23.0 %all-to-all-start.1 = ((s32[64,1,128]{2,1,0:T(1,128)}), s32[64,1,128]{2,1,0:T(1,128)S(1)}, u32[]{:S(2)}, u32[]{:S(2)}) async-start(s32[64,1,128]{2,1,0:T(1,128)} %get-tuple-element.26), calls=%async_computation.1 | async-start | bytes 65536 | tf_op jit(solution)/shard_map/all_to_all | solution.py:281
  36.9 14.1 %copy-start = (s32[1024,1]{0,1:T(1,128)S(1)}, s32[1024,1]{0,1:T(1,128)}, u32[]{:S(2)}) copy-start(s32[1024,1]{0,1:T(1,128)} %param.10) | copy-start | bytes 12292

commit v5 on v4

--- a/solution.py
+++ b/solution.py
@@ -149,7 +149,7 @@
 
 def serve_kernel(packed_ref, request_ref, answer_ref, turned_ref, tables_ref):
     for s in range(8):
-        tables_ref[s] = packed_ref[s].astype(F32)
+        tables_ref[s * NV * 16 : (s + 1) * NV * 16, :] = packed_ref[s].astype(F32)
     turned_ref[...] = jnp.transpose(request_ref[...].reshape(64, 128).astype(F32), (1, 0))
     lane = iota((8, 128), 1)
     lane_block = lane // SLOTS
@@ -169,7 +169,7 @@
     for k in range(16):
         here = [h == k for h in high]
         for v in range(NV):
-            piece = tables_ref[:, v * 16 + k, :]
+            piece = tables_ref[pl.ds(v * 16 + k, 8, stride=NV * 16), :]
             for c in range(4):
                 got = jnp.take_along_axis(piece, low[c], axis=1)
                 looked_up[c][v] = jnp.where(here[c], got, looked_up[c][v])
@@ -258,7 +258,7 @@
 def serve(tables, requests):
     return pl.pallas_call(
         serve_kernel, out_shape=shape((256, 128), BF16),
-        scratch_shapes=[pltpu.VMEM((128, 64), F32), pltpu.VMEM((8, NV * 16, 128), F32)],
+        scratch_shapes=[pltpu.VMEM((128, 64), F32), pltpu.VMEM((8 * NV * 16, 128), F32)],
         compiler_params=SMALL, name="serve",
     )(tables, requests)
 

time: 52.4 us -> 52.4 us (level)
  no operation moved by 1% of the time
where the time goes in v5:
time: 52.4 us; the launch traced here: 51.9 us
  blocking collectives  23.8 us (45%)
  starting transfers between devices  19.2 us (37%)
  Pallas kernels  8.19 us (16%)
  between operations  0.68 us (1%)
    all_to_all x1, starting transfers between devices, body(): lax.all_to_all(requests, FAR, 0, 0, axis_index_groups=listed(64, ASK), ti...  19.2 us
    all_to_all x1, blocking collectives, body(): lax.all_to_all(answers, FAR, 0, 0, axis_index_groups=listed(64, REPLY), t...  14 us
    all_to_all x1, blocking collectives, body(): lax.all_to_all(table, SIDE, 0, 0, axis_index_groups=listed(8, SHARE), til...  9.76 us
    pallas_call x1, Pallas kernels, critics(): pl.pallas_call(critic_kernel, out_shape=shape((8, NV * 16, 128), BF16), s...  3.72 us
    pallas_call x1, Pallas kernels, make_request(): pl.pallas_call(request_kernel, in_specs=[pl.BlockSpec(memory_space=pl.ANY...  2.16 us
    pallas_call x1, Pallas kernels, serve(): pl.pallas_call(serve_kernel, out_shape=shape((256, 128), BF16), scratch_s...  1.38 us
  transfers between devices with their start and end apart: 1, of which 0 were waited for; matrix products, arithmetic and copies ran while one was open for 0% of the time, Pallas kernels for 7%

profile of v5, /device:TPU:1, one launch (start us, length us, event | category | flops | bytes accessed | tf_op | source)
XLA Modules:
  0.0 51.9 jit_solution(10915977633929514080)
XLA Ops:
  0.6 2.2 %make_request.1 = (s32[64,1,128]{2,1,0:T(1,128)}, s32[8,128]{1,0:T(8,128)S(1)}, bf16[2048,256]{1,0:T(8,128)(2,1)S(1)}, bf16[130,2,256]{2,1,0:T(2,128)(2,1)S(1)},...) custom-call(s32[8,128]{1,0:T(8,128)} %bitcast.10, ...), custom_call_target="tpu_custom_call" | custom-call | tf_op jit(solution)/shard_map/make_request/pallas_call | solution.py:227
  2.8 19.2 %all-to-all-start.1 = ((s32[64,1,128]{2,1,0:T(1,128)}), s32[64,1,128]{2,1,0:T(1,128)S(1)}, u32[]{:S(2)}, u32[]{:S(2)}) async-start(s32[64,1,128]{2,1,0:T(1,128)} %get-tuple-element.26), calls=%async_computation.1 | async-start | bytes 65536 | tf_op jit(solution)/shard_map/all_to_all | solution.py:281
  22.1 3.7 %critics.1 = bf16[8,112,128]{2,1,0:T(8,128)(2,1)S(1)} custom-call(bf16[2048,256]{1,0:T(8,128)(2,1)S(1)} %get-tuple-element.19.rows_ref, bf16[130,2,256]{2,1,0:T(2,128)(2,1)S(1)} %get-tuple-element.20.q_in_ref, bf16[2,256,256]{2,1,0:T(8,128)(2,1)S(1)} %get-tuple-element.21.q_mid_ref, bf16[124,256]{1,0:T(8,128)(2,1)S(1)} %get-tuple-element.22.v_in_ref, ...), custom_call_target="tpu_custom_call" | custom-call | flops 2147483648 | bytes 2000000 | tf_op jit(solution)/shard_map/critics/pallas_call | solution.py:244
  25.8 0.0 all-to-all-done.1.request_ref
  25.8 9.8 %all_to_all.15.packed_ref = bf16[8,112,128]{2,1,0:T(8,128)(2,1)S(1)} all-to-all(bf16[8,112,128]{2,1,0:T(8,128)(2,1)S(1)} %critics.1), channel_id=1, replica_groups={{33,32,49,48,1,0,17,16},{35,34,51,50,3,2,19,18},{37,36,53,52,5,4,21,20}..., dimensions={0} | all-to-all | bytes 458752 | tf_op jit(solution)/shard_map/all_to_all | solution.py:283
  35.5 1.4 %serve.1 = bf16[256,128]{1,0:T(8,128)(2,1)S(1)} custom-call(bf16[8,112,128]{2,1,0:T(8,128)(2,1)S(1)} %all_to_all.15.packed_ref, s32[64,1,128]{2,1,0:T(1,128)S(1)} %all-to-all-done.1.request_ref), custom_call_target="tpu_custom_call" | custom-call | tf_op jit(solution)/shard_map/serve/pallas_call | solution.py:259
  36.9 0.0 copy-start
  36.9 14.0 %all_to_all.16 = bf16[64,4,128]{2,1,0:T(4,128)(2,1)S(1)} all-to-all(bf16[64,4,128]{2,1,0:T(4,128)(2,1)S(1)} %bitcast.8), channel_id=1, replica_groups={{264,266,268,270,256,258,260,262,328,330,332,334,320,322,324,326,392,39..., dimensions={0} | all-to-all | bytes 131072 | tf_op jit(solution)/shard_map/all_to_all | solution.py:285
  51.0 0.0 copy-done
  51.0 0.9 %finish.1 = (f32[2,1024]{1,0:T(2,128)}, f32[2,1024]{1,0:T(2,128)}, f32[1,1024]{1,0:T(1,128)}, f32[1,1024]{1,0:T(1,128)}, f32[1,1024]{1,0:T(1,128)}) custom-call(bf16[256,128]{1,0:T(8,128)(2,1)S(1)} %bitcast.9, s32[8,128]{1,0:T(8,128)S(1)} %bitcast.11, s32[8,128]{1,0:T(8,128)S(1)} %get-tuple-element.27.rank_ref), custom_call_target="tpu_custom_call" | custom-call | tf_op jit(solution)/shard_map/finish/pallas_call | solution.py:269
Async XLA Ops:
  2.8 23.0 %all-to-all-start.1 = ((s32[64,1,128]{2,1,0:T(1,128)}), s32[64,1,128]{2,1,0:T(1,128)S(1)}, u32[]{:S(2)}, u32[]{:S(2)}) async-start(s32[64,1,128]{2,1,0:T(1,128)} %get-tuple-element.26), calls=%async_computation.1 | async-start | bytes 65536 | tf_op jit(solution)/shard_map/all_to_all | solution.py:281
  36.9 14.1 %copy-start = (s32[1024,1]{0,1:T(1,128)S(1)}, s32[1024,1]{0,1:T(1,128)}, u32[]{:S(2)}) copy-start(s32[1024,1]{0,1:T(1,128)} %param.10) | copy-start | bytes 12292
